TPU v7x, 512 devices: a whole 4x4x16 slice. The times are simulated.
512 devices in a mesh: dp: 8 (over z_lo), row: 16 (over z_hi, x, core), col: 4 (over y).
Axes of the slice: x: 4, y: 4, z: 16 (z_hi: 2, z_lo: 8; z = z_hi * 8 + z_lo), core: 2. Of those that a mesh axis runs over, the one named last changes fastest.
Arguments:
- expand_gradient: bfloat16 [8, 4096, 5120], P('dp', 'row', 'col'), may hold values from -24 to 24, as said below
- expand_master: float32 [4096, 5120], P(('row', 'dp'), 'col'), may hold values from -0.12 to 0.12
- expand_rows: float32 [4096], P(('row', 'dp')), may hold values from 0.01 to 1
- expand_columns: float32 [5120], P('col'), may hold values from 0.01 to 1
- contract_gradient: bfloat16 [8, 5120, 4096], P('dp', 'row', 'col'), may hold values from -24 to 24, as said below
- contract_master: float32 [5120, 4096], P(('row', 'dp'), 'col'), may hold values from -0.12 to 0.12
- contract_rows: float32 [5120], P(('row', 'dp')), may hold values from 0.01 to 1
- contract_columns: float32 [4096], P('col'), may hold values from 0.01 to 1
- attend_gradient: bfloat16 [8, 4096, 4096], P('dp', 'row', 'col'), may hold values from -24 to 24, as said below
- attend_master: float32 [4096, 4096], P(('row', 'dp'), 'col'), may hold values from -0.12 to 0.12
- attend_rows: float32 [4096], P(('row', 'dp')), may hold values from 0.01 to 1
- attend_columns: float32 [4096], P('col'), may hold values from 0.01 to 1
Outputs:
- expand_updated: float32 [4096, 5120], P(('row', 'dp'), 'col')
- expand_weights: bfloat16 [4096, 5120], P('row', 'col')
- expand_rows_next: float32 [4096], P(('row', 'dp'))
- expand_columns_next: float32 [5120], P('col')
- expand_step: float32 [4096, 5120], P(('row', 'dp'), 'col')
- contract_updated: float32 [5120, 4096], P(('row', 'dp'), 'col')
- contract_weights: bfloat16 [5120, 4096], P('row', 'col')
- contract_rows_next: float32 [5120], P(('row', 'dp'))
- contract_columns_next: float32 [4096], P('col')
- contract_step: float32 [5120, 4096], P(('row', 'dp'), 'col')
- attend_updated: float32 [4096, 4096], P(('row', 'dp'), 'col')
- attend_weights: bfloat16 [4096, 4096], P('row', 'col')
- attend_rows_next: float32 [4096], P(('row', 'dp'))
- attend_columns_next: float32 [4096], P('col')
- attend_step: float32 [4096, 4096], P(('row', 'dp'), 'col')
Inputs may be any that keep to these rules, and one draw needn't show every extreme that they name: `expand_gradient`: each replica's gradient, of any scale from entry to entry. `contract_gradient`: each replica's gradient, of any scale from entry to entry. `attend_gradient`: each replica's gradient, of any scale from entry to entry.
All inputs are finite; a program needn't handle non-finite values.
Results may differ from a plain program's by a relative error of at most 0.0004.
Values may be sent and summed in bfloat16 or wider, within the bound.
A program may use at most 64 MiB of HBM per device.

v0:
```python
import jax
import jax.numpy as jnp
from jax import lax
from jax.sharding import Mesh
from jax.sharding import PartitionSpec as P

ROW = ("row_0", "row_1", "row_2")
DP_ROW = ("dp", "row_0", "row_1", "row_2")
DP_ROW_COL = ("dp", "row_0", "row_1", "row_2", "col")
ROW_DP = ("row_0", "row_1", "row_2", "dp")


tiny_square = 1e-30
decay_rate = 0.9
learn_rate = 0.01


def in_order(blocks, dim):
    blocks = jnp.moveaxis(blocks, 0, dim)
    lengths = blocks.shape
    return blocks.reshape(*lengths[:dim], lengths[dim] * lengths[dim + 1], *lengths[dim + 2 :])


def from_everyone(shard, axis):
    copies = jnp.broadcast_to(shard, (lax.axis_size(axis), *shard.shape))
    return lax.all_to_all(copies, axis, split_axis=0, concat_axis=0, tiled=True)


def collect(shard, axis, dim):
    return in_order(from_everyone(shard, axis), dim)


def taken_together(shard, axis):
    everything = from_everyone(shard, axis)
    return jnp.sum(everything, axis=0)


def packed_total(arrays, axis):
    ends = [0]
    for a in arrays:
        ends.append(ends[-1] + a.size)
    subtotal = taken_together(jnp.concatenate([a.ravel() for a in arrays]), axis)
    return tuple((subtotal[b:e].reshape(a.shape) for a, b, e in zip(arrays, ends, ends[1:])))


def one_axis_at_a_time(shard, axes):
    for axis in axes:
        shard = lax.psum(shard, axis)
    return shard


def finish(update_raw, clip_total, master, full_size):
    clip_scale = jnp.maximum(1.0, jnp.sqrt(clip_total / full_size))
    step_taken = update_raw / clip_scale
    updated = master - learn_rate * step_taken
    weights = collect(updated.astype(jnp.bfloat16), "dp", 0)
    return (updated, weights, step_taken)


def reduce_gradient(gradient, dp_count):
    received = lax.all_to_all(gradient, "dp", split_axis=1, concat_axis=0, tiled=True)
    summed = jnp.sum(received.astype(jnp.float32), axis=0)
    return summed / dp_count


def body(
    expand_gradient,
    expand_master,
    expand_rows,
    expand_columns,
    contract_gradient,
    contract_master,
    contract_rows,
    contract_columns,
    attend_gradient,
    attend_master,
    attend_rows,
    attend_columns,
):
    groups = (
        (expand_gradient, expand_master, expand_rows, expand_columns),
        (contract_gradient, contract_master, contract_rows, contract_columns),
        (attend_gradient, attend_master, attend_rows, attend_columns),
    )
    dp_count = lax.axis_size("dp")
    col_count = lax.axis_size("col")
    split_count = dp_count * lax.axis_size(ROW)
    means = []
    for gradient, master, row_stat, column_stat in groups:
        means.append(reduce_gradient(gradient, dp_count))
    squares = [mean_grad * mean_grad + tiny_square for mean_grad in means]
    row_parts = [jnp.sum(square_block, axis=1) for square_block in squares]
    column_parts = [jnp.sum(square_block, axis=0) for square_block in squares]
    heights = [mean_grad.shape[0] * split_count for mean_grad in means]
    widths = [mean_grad.shape[1] * col_count for mean_grad in means]
    outputs = []
    row_totals = packed_total((row_parts[0], row_parts[1], row_parts[2]), "col")
    rows_next = [
        decay_rate * groups[which][2] + (1.0 - decay_rate) * row_totals[which] / widths[which]
        for which in range(3)
    ]
    joined = (
        one_axis_at_a_time(column_parts[0], DP_ROW),
        one_axis_at_a_time(column_parts[1], DP_ROW),
        one_axis_at_a_time(column_parts[2], DP_ROW),
        one_axis_at_a_time(jnp.sum(rows_next[0]), DP_ROW),
        one_axis_at_a_time(jnp.sum(rows_next[1]), DP_ROW),
        one_axis_at_a_time(jnp.sum(rows_next[2]), DP_ROW),
    )
    columns_next = [
        decay_rate * groups[which][3] + (1.0 - decay_rate) * joined[which] / heights[which]
        for which in range(3)
    ]
    raws = [
        means[which]
        * jnp.sqrt(
            joined[3 + which]
            / heights[which]
            / (rows_next[which][:, None] * columns_next[which][None, :])
        )
        for which in range(3)
    ]
    clips = (
        one_axis_at_a_time(jnp.sum(raws[0] * raws[0]), DP_ROW_COL),
        one_axis_at_a_time(jnp.sum(raws[1] * raws[1]), DP_ROW_COL),
        one_axis_at_a_time(jnp.sum(raws[2] * raws[2]), DP_ROW_COL),
    )
    for which in range(3):
        updated, weights, step_taken = finish(
            raws[which], clips[which], groups[which][1], heights[which] * widths[which]
        )
        outputs.extend([updated, weights, rows_next[which], columns_next[which], step_taken])
    return tuple(outputs)


def solution(mesh):
    finer = Mesh(
        mesh.devices.reshape(mesh.shape["dp"], 2, 4, 2, mesh.shape["col"]),
        ("dp", "row_0", "row_1", "row_2", "col"),
    )
    in_specs = (
        P("dp", ROW, "col"),
        P(ROW_DP, "col"),
        P(ROW_DP),
        P("col"),
        P("dp", ROW, "col"),
        P(ROW_DP, "col"),
        P(ROW_DP),
        P("col"),
        P("dp", ROW, "col"),
        P(ROW_DP, "col"),
        P(ROW_DP),
        P("col"),
    )
    out_specs = (
        P(ROW_DP, "col"),
        P(ROW, "col"),
        P(ROW_DP),
        P("col"),
        P(ROW_DP, "col"),
        P(ROW_DP, "col"),
        P(ROW, "col"),
        P(ROW_DP),
        P("col"),
        P(ROW_DP, "col"),
        P(ROW_DP, "col"),
        P(ROW, "col"),
        P(ROW_DP),
        P("col"),
        P(ROW_DP, "col"),
    )
    return jax.shard_map(body, mesh=finer, in_specs=in_specs, out_specs=out_specs, check_vma=False)
```

profile of v0, /device:TPU:6, one launch (start us, length us, event | category | flops | bytes accessed | tf_op | source)
XLA Modules:
  0.0 414.5 jit_solution(8251407359261963405)
XLA Ops:
  0.6 1.9 copy.54
  3.0 3.7 reduce.2
  6.7 1.2 reshape.72
  7.9 12.5 %all-to-all-start.2 = ((bf16[8,2,16384]{2,1,0:T(2,128)(2,1)}), bf16[8,2,16384]{2,1,0:T(2,128)(2,1)S(1)}, u32[]{:S(2)}, u32[]{:S(2)}) async-start(bf16[8,2,16384]{2,1,0:T(2,128)(2,1)} %reshape.72), calls=%async_computation.2 | async-start | bytes 1048576 | tf_op jit(solution)/shard_map/all_to_all | solution.py:61
  20.4 1.0 copy.53
  21.4 4.6 %reduce.1 = bf16[256,1280]{1,0:T(8,128)(2,1)S(1)} reduce(bf16[256,1,1280]{2,1,0:T(2,128)(2,1)S(1)} %bitcast.23, bf16[]{:T(256)} %broadcast.40), dimensions={1}, to_apply=%bitcast.20.reduce_sub_computation | reduce | bytes 1310722
  26.1 1.0 reshape.70
  27.1 22.1 %all-to-all-done.2 = bf16[8,2,16384]{2,1,0:T(2,128)(2,1)S(1)} async-done(((bf16[8,2,16384]{2,1,0:T(2,128)(2,1)}), bf16[8,2,16384]{2,1,0:T(2,128)(2,1)S(1)}, u32[]{:S(2)}, u32[]{:S(2)}) %all-to-all-start.2) | async-done | bytes 524320 | tf_op jit(solution)/shard_map/all_to_all | solution.py:61
  49.9 4.3 %all-to-all-start = ((bf16[8,2,20480]{2,1,0:T(2,128)(2,1)}), bf16[8,2,20480]{2,1,0:T(2,128)(2,1)S(1)}, u32[]{:S(2)}, u32[]{:S(2)}) async-start(bf16[8,2,20480]{2,1,0:T(2,128)(2,1)} %reshape.70), calls=%async_computation | async-start | bytes 1310720 | tf_op jit(solution)/shard_map/all_to_all | solution.py:61
  54.2 1.0 copy.52
  55.2 4.5 %reduce.3 = bf16[320,1024]{1,0:T(8,128)(2,1)S(1)} reduce(bf16[320,1,1024]{2,1,0:T(2,128)(2,1)S(1)} %bitcast.22, bf16[]{:T(256)} %broadcast.40), dimensions={1}, to_apply=%bitcast.19.reduce_sub_computation | reduce | bytes 1310722
  59.7 1.3 reshape.74
  61.0 27.3 %all-to-all-done = bf16[8,2,20480]{2,1,0:T(2,128)(2,1)S(1)} async-done(((bf16[8,2,20480]{2,1,0:T(2,128)(2,1)}), bf16[8,2,20480]{2,1,0:T(2,128)(2,1)S(1)}, u32[]{:S(2)}, u32[]{:S(2)}) %all-to-all-start) | async-done | bytes 655392 | tf_op jit(solution)/shard_map/all_to_all | solution.py:61
  88.2 4.3 %all-to-all-start.1 = ((bf16[8,2,20480]{2,1,0:T(2,128)(2,1)}), bf16[8,2,20480]{2,1,0:T(2,128)(2,1)S(1)}, u32[]{:S(2)}, u32[]{:S(2)}) async-start(bf16[8,2,20480]{2,1,0:T(2,128)(2,1)} %reshape.74), calls=%async_computation.1 | async-start | bytes 1310720 | tf_op jit(solution)/shard_map/all_to_all | solution.py:61
  94.4 31.9 %all-to-all-done.1 = bf16[8,2,20480]{2,1,0:T(2,128)(2,1)S(1)} async-done(((bf16[8,2,20480]{2,1,0:T(2,128)(2,1)}), bf16[8,2,20480]{2,1,0:T(2,128)(2,1)S(1)}, u32[]{:S(2)}, u32[]{:S(2)}) %all-to-all-start.1) | async-done | bytes 655392 | tf_op jit(solution)/shard_map/all_to_all | solution.py:61
  127.7 9.5 %all_to_all.48 = f32[4,1,104]{2,1,0:T(1,128)S(1)} all-to-all(f32[4,1,104]{2,1,0:T(1,128)S(1)} %broadcast_in_dim.8), channel_id=1, replica_groups=mesh['dp'=8,'row_0'=2,'row_1'=4,'row_2'=2,'col'=4] {'col'}, dimensions={0} | all-to-all | bytes 3328 | tf_op jit(solution)/shard_map/all_to_all | solution.py:26
  138.6 52.8 %all-reduce.1 = (f32[1280]{0:T(1024)S(1)}, f32[]{:T(128)}, f32[1024]{0:T(1024)S(1)}, f32[]{:T(128)}, f32[1024]{0:T(1024)S(1)}, /*index=5*/f32[]{:T(128)}) all-reduce(f32[1280]{0:T(1024)S(1)} %get-tuple-element.18, f32[]{:T(128)} %get-tuple-element.75, ...), channel_id=1, replica_groups=mesh['dp'=8,'row_0'=2,'row_1'=4,'row_2'=2,'col'=4] {'dp'}, use_global_device_ids=true, to_apply=%region_13.0 | all-reduce | flops 3331 | bytes 26648 | tf_op jit(solution)/shard_map/psum | solution.py:48
  191.4 23.0 %all-reduce.8 = (f32[1280]{0:T(1024)S(1)}, f32[]{:T(128)}, f32[1024]{0:T(1024)S(1)}, f32[]{:T(128)}, f32[1024]{0:T(1024)S(1)}, /*index=5*/f32[]{:T(128)}) all-reduce(f32[1280]{0:T(1024)S(1)} %get-tuple-element.24, f32[]{:T(128)} %get-tuple-element.25, ...), channel_id=1, replica_groups=mesh['dp'=8,'row_0'=2,'row_1'=4,'row_2'=2,'col'=4] {'row_0'}, use_global_device_ids=true, to_apply=%region_14.0 | all-reduce | flops 3331 | bytes 26648 | tf_op jit(solution)/shard_map/psum | solution.py:48
  214.4 15.1 %all-reduce.4 = (f32[1280]{0:T(1024)S(1)}, f32[]{:T(128)}, f32[1024]{0:T(1024)S(1)}, f32[]{:T(128)}, f32[1024]{0:T(1024)S(1)}, /*index=5*/f32[]{:T(128)}) all-reduce(f32[1280]{0:T(1024)S(1)} %get-tuple-element.54, f32[]{:T(128)} %get-tuple-element.55, ...), channel_id=1, replica_groups=mesh['dp'=8,'row_0'=2,'row_1'=4,'row_2'=2,'col'=4] {'row_1'}, use_global_device_ids=true, to_apply=%region_15.0 | all-reduce | flops 3331 | bytes 26648 | tf_op jit(solution)/shard_map/psum | solution.py:48
  229.5 4.5 %all-reduce.6 = (f32[1280]{0:T(1024)S(1)}, f32[]{:T(128)}, f32[1024]{0:T(1024)S(1)}, f32[]{:T(128)}, f32[1024]{0:T(1024)S(1)}, /*index=5*/f32[]{:T(128)}) all-reduce(f32[1280]{0:T(1024)S(1)} %get-tuple-element.36, f32[]{:T(128)} %get-tuple-element.37, ...), channel_id=1, replica_groups=mesh['dp'=8,'row_0'=2,'row_1'=4,'row_2'=2,'col'=4] {'row_2'}, use_global_device_ids=true, to_apply=%region_16.0 | all-reduce | flops 3331 | bytes 26648 | tf_op jit(solution)/shard_map/psum | solution.py:48
  238.3 25.7 %all-reduce = (f32[]{:T(128)}, f32[]{:T(128)}, f32[]{:T(128)}) all-reduce(f32[]{:T(128)} %multiply_reduce_fusion.1, f32[]{:T(128)} %multiply_reduce_fusion, f32[]{:T(128)} %multiply_reduce_fusion.2), channel_id=1, replica_groups=mesh['dp'=8,'row_0'=2,'row_1'=4,'row_2'=2,'col'=4] {'dp'}, use_global_device_ids=true, to_apply=%region_18.0 | all-reduce | flops 3 | bytes 24 | tf_op jit(solution)/shard_map/psum | solution.py:48
  263.9 14.3 %all-reduce.7 = (f32[]{:T(128)}, f32[]{:T(128)}, f32[]{:T(128)}) all-reduce(f32[]{:T(128)} %get-tuple-element.21, f32[]{:T(128)} %get-tuple-element.22, f32[]{:T(128)} %get-tuple-element.23), channel_id=1, replica_groups=mesh['dp'=8,'row_0'=2,'row_1'=4,'row_2'=2,'col'=4] {'row_0'}, use_global_device_ids=true, to_apply=%region_19.0 | all-reduce | flops 3 | bytes 24 | tf_op jit(solution)/shard_map/psum | solution.py:48
  278.2 10.6 %all-reduce.3 = (f32[]{:T(128)}, f32[]{:T(128)}, f32[]{:T(128)}) all-reduce(f32[]{:T(128)} %get-tuple-element.51, f32[]{:T(128)} %get-tuple-element.52, f32[]{:T(128)} %get-tuple-element.53), channel_id=1, replica_groups=mesh['dp'=8,'row_0'=2,'row_1'=4,'row_2'=2,'col'=4] {'row_1'}, use_global_device_ids=true, to_apply=%region_20.0 | all-reduce | flops 3 | bytes 24 | tf_op jit(solution)/shard_map/psum | solution.py:48
  288.8 3.1 all-reduce.5
  291.9 9.5 %all-reduce.2 = (f32[]{:T(128)}, f32[]{:T(128)}, f32[]{:T(128)}) all-reduce(f32[]{:T(128)} %get-tuple-element.42, f32[]{:T(128)} %get-tuple-element.43, f32[]{:T(128)} %get-tuple-element.44), channel_id=1, replica_groups=mesh['dp'=8,'row_0'=2,'row_1'=4,'row_2'=2,'col'=4] {'col'}, use_global_device_ids=true, to_apply=%region_22.0 | all-reduce | flops 3 | bytes 24 | tf_op jit(solution)/shard_map/psum | solution.py:48
  303.8 3.5 all-to-all-start.6
  308.9 25.6 %all-to-all-done.6 = bf16[8,32,1024]{2,1,0:T(8,128)(2,1)S(1)} async-done(((bf16[8,32,1024]{2,1,0:T(8,128)(2,1)}), bf16[8,32,1024]{2,1,0:T(8,128)(2,1)S(1)}, u32[]{:S(2)}, u32[]{:S(2)}) %all-to-all-start.6) | async-done | bytes 524320 | tf_op jit(solution)/shard_map/all_to_all | solution.py:26
  335.4 4.3 %all-to-all-start.4 = ((bf16[8,32,1280]{2,1,0:T(8,128)(2,1)}), bf16[8,32,1280]{2,1,0:T(8,128)(2,1)S(1)}, u32[]{:S(2)}, u32[]{:S(2)}) async-start(bf16[8,32,1280]{2,1,0:T(8,128)(2,1)} %broadcast_in_dim.9), calls=%async_computation.4 | async-start | bytes 1310720 | tf_op jit(solution)/shard_map/all_to_all | solution.py:26
  341.3 32.0 %all-to-all-done.4 = bf16[8,32,1280]{2,1,0:T(8,128)(2,1)S(1)} async-done(((bf16[8,32,1280]{2,1,0:T(8,128)(2,1)}), bf16[8,32,1280]{2,1,0:T(8,128)(2,1)S(1)}, u32[]{:S(2)}, u32[]{:S(2)}) %all-to-all-start.4) | async-done | bytes 655392 | tf_op jit(solution)/shard_map/all_to_all | solution.py:26
  373.3 0.9 broadcast_in_dim.20
  374.3 4.3 %all-to-all-start.5 = ((bf16[8,40,1024]{2,1,0:T(8,128)(2,1)}), bf16[8,40,1024]{2,1,0:T(8,128)(2,1)S(1)}, u32[]{:S(2)}, u32[]{:S(2)}) async-start(bf16[8,40,1024]{2,1,0:T(8,128)(2,1)} %broadcast_in_dim.20), calls=%async_computation.5 | async-start | bytes 1310720 | tf_op jit(solution)/shard_map/all_to_all | solution.py:26
  378.6 33.5 %all-to-all-done.5 = bf16[8,40,1024]{2,1,0:T(8,128)(2,1)S(1)} async-done(((bf16[8,40,1024]{2,1,0:T(8,128)(2,1)}), bf16[8,40,1024]{2,1,0:T(8,128)(2,1)S(1)}, u32[]{:S(2)}, u32[]{:S(2)}) %all-to-all-start.5) | async-done | bytes 655392 | tf_op jit(solution)/shard_map/all_to_all | solution.py:26
  (69 shorter events, 14.9 us)
Async XLA Ops:
  6.7 13.7 %copy-start.2 = (bf16[1,256,1280]{2,1,0:T(8,128)(2,1)S(1)}, bf16[1,256,1280]{2,1,0:T(8,128)(2,1)}, u32[]{:S(2)}) copy-start(bf16[1,256,1280]{2,1,0:T(8,128)(2,1)} %param.12) | copy-start | bytes 1966084
  7.9 41.3 %all-to-all-start.2 = ((bf16[8,2,16384]{2,1,0:T(2,128)(2,1)}), bf16[8,2,16384]{2,1,0:T(2,128)(2,1)S(1)}, u32[]{:S(2)}, u32[]{:S(2)}) async-start(bf16[8,2,16384]{2,1,0:T(2,128)(2,1)} %reshape.72), calls=%async_computation.2 | async-start | bytes 1048576 | tf_op jit(solution)/shard_map/all_to_all | solution.py:61
  26.1 28.1 %copy-start.3 = (bf16[1,320,1024]{2,1,0:T(8,128)(2,1)S(1)}, bf16[1,320,1024]{2,1,0:T(8,128)(2,1)}, u32[]{:S(2)}) copy-start(bf16[1,320,1024]{2,1,0:T(8,128)(2,1)} %param.16) | copy-start | bytes 1966084
  49.2 0.8 copy-start
  49.9 38.3 %all-to-all-start = ((bf16[8,2,20480]{2,1,0:T(2,128)(2,1)}), bf16[8,2,20480]{2,1,0:T(2,128)(2,1)S(1)}, u32[]{:S(2)}, u32[]{:S(2)}) async-start(bf16[8,2,20480]{2,1,0:T(2,128)(2,1)} %reshape.70), calls=%async_computation | async-start | bytes 1310720 | tf_op jit(solution)/shard_map/all_to_all | solution.py:61
  61.0 31.6 %copy-start.1 = (bf16[8,2,16384]{2,1,0:T(2,128)(2,1)S(1)}, bf16[8,2,16384]{2,1,0:T(2,128)(2,1)}, u32[]{:S(2)}) copy-start(bf16[8,2,16384]{2,1,0:T(2,128)(2,1)} %copy-done) | copy-start | bytes 1572868
  88.2 38.2 %all-to-all-start.1 = ((bf16[8,2,20480]{2,1,0:T(2,128)(2,1)}), bf16[8,2,20480]{2,1,0:T(2,128)(2,1)S(1)}, u32[]{:S(2)}, u32[]{:S(2)}) async-start(bf16[8,2,20480]{2,1,0:T(2,128)(2,1)} %reshape.74), calls=%async_computation.1 | async-start | bytes 1310720 | tf_op jit(solution)/shard_map/all_to_all | solution.py:61
  127.0 10.2 %copy-start.16 = (f32[40]{0:T(128)S(1)}, f32[40]{0:T(128)}, u32[]{:S(2)}) copy-start(f32[40]{0:T(128)} %param.18) | copy-start | bytes 484
  127.0 10.9 %copy-start.17 = (f32[32]{0:T(128)S(1)}, f32[32]{0:T(128)}, u32[]{:S(2)}) copy-start(f32[32]{0:T(128)} %param.22) | copy-start | bytes 388
  127.0 10.8 %copy-start.18 = (f32[32]{0:T(128)S(1)}, f32[32]{0:T(128)}, u32[]{:S(2)}) copy-start(f32[32]{0:T(128)} %param.14) | copy-start | bytes 388
  127.1 108.2 %copy-start.10 = (f32[1280]{0:T(1024)S(1)}, f32[1280]{0:T(1024)}, u32[]{:S(2)}) copy-start(f32[1280]{0:T(1024)} %param.15) | copy-start | bytes 15364
  127.1 109.7 %copy-start.14 = (f32[1024]{0:T(1024)S(1)}, f32[1024]{0:T(1024)}, u32[]{:S(2)}) copy-start(f32[1024]{0:T(1024)} %param.23) | copy-start | bytes 12292
  127.1 109.7 %copy-start.15 = (f32[1024]{0:T(1024)S(1)}, f32[1024]{0:T(1024)}, u32[]{:S(2)}) copy-start(f32[1024]{0:T(1024)} %param.19) | copy-start | bytes 12292
  127.3 174.8 %copy-start.6 = (f32[32,1024]{1,0:T(8,128)S(1)}, f32[32,1024]{1,0:T(8,128)}, u32[]{:S(2)}) copy-start(f32[32,1024]{1,0:T(8,128)} %param.21) | copy-start | bytes 393220
  137.9 202.5 %copy-start.11 = (f32[40]{0:T(128)}, f32[40]{0:T(128)S(1)}, u32[]{:S(2)}) copy-start(f32[40]{0:T(128)S(1)} %get-tuple-element.101) | copy-start | bytes 484
  138.6 165.2 %copy-start.13 = (f32[32]{0:T(128)}, f32[32]{0:T(128)S(1)}, u32[]{:S(2)}) copy-start(f32[32]{0:T(128)S(1)} %get-tuple-element.106) | copy-start | bytes 388
  138.6 169.4 %copy-start.12 = (f32[32]{0:T(128)}, f32[32]{0:T(128)S(1)}, u32[]{:S(2)}) copy-start(f32[32]{0:T(128)S(1)} %get-tuple-element.96) | copy-start | bytes 388
  235.3 72.7 %copy-start.7 = (f32[1280]{0:T(1024)}, f32[1280]{0:T(1024)S(1)}, u32[]{:S(2)}) copy-start(f32[1280]{0:T(1024)S(1)} %multiply_add_fusion.3) | copy-start | bytes 15364
  236.7 71.3 %copy-start.4 = (f32[32,1280]{1,0:T(8,128)S(1)}, f32[32,1280]{1,0:T(8,128)}, u32[]{:S(2)}) copy-start(f32[32,1280]{1,0:T(8,128)} %param.13) | copy-start | bytes 491524
  236.7 72.2 %copy-start.8 = (f32[1024]{0:T(1024)}, f32[1024]{0:T(1024)S(1)}, u32[]{:S(2)}) copy-start(f32[1024]{0:T(1024)S(1)} %get-tuple-element.107) | copy-start | bytes 12292
  236.8 103.7 %copy-start.9 = (f32[1024]{0:T(1024)}, f32[1024]{0:T(1024)S(1)}, u32[]{:S(2)}) copy-start(f32[1024]{0:T(1024)S(1)} %get-tuple-element.102) | copy-start | bytes 12292
  303.8 30.7 %all-to-all-start.6 = ((bf16[8,32,1024]{2,1,0:T(8,128)(2,1)}), bf16[8,32,1024]{2,1,0:T(8,128)(2,1)S(1)}, u32[]{:S(2)}, u32[]{:S(2)}) async-start(bf16[8,32,1024]{2,1,0:T(8,128)(2,1)} %broadcast_in_dim.21), calls=%async_computation.6 | async-start | bytes 1048576 | tf_op jit(solution)/shard_map/all_to_all | solution.py:26
  308.0 32.4 %copy-start.5 = (f32[40,1024]{1,0:T(8,128)S(1)}, f32[40,1024]{1,0:T(8,128)}, u32[]{:S(2)}) copy-start(f32[40,1024]{1,0:T(8,128)} %param.17) | copy-start | bytes 491524
  335.4 37.9 %all-to-all-start.4 = ((bf16[8,32,1280]{2,1,0:T(8,128)(2,1)}), bf16[8,32,1280]{2,1,0:T(8,128)(2,1)S(1)}, u32[]{:S(2)}, u32[]{:S(2)}) async-start(bf16[8,32,1280]{2,1,0:T(8,128)(2,1)} %broadcast_in_dim.9), calls=%async_computation.4 | async-start | bytes 1310720 | tf_op jit(solution)/shard_map/all_to_all | solution.py:26
  374.3 37.8 %all-to-all-start.5 = ((bf16[8,40,1024]{2,1,0:T(8,128)(2,1)}), bf16[8,40,1024]{2,1,0:T(8,128)(2,1)S(1)}, u32[]{:S(2)}, u32[]{:S(2)}) async-start(bf16[8,40,1024]{2,1,0:T(8,128)(2,1)} %broadcast_in_dim.20), calls=%async_computation.5 | async-start | bytes 1310720 | tf_op jit(solution)/shard_map/all_to_all | solution.py:26
where the time goes:
time: 417 us; the launch traced here: 414 us
  waiting for transfers between devices  172 us (41%)
  blocking collectives  168 us (40%)
  starting transfers between devices  33.2 us (8%)
  other arithmetic  19.8 us (5%)
  local copies, waits for them, and re-layouts  16.1 us (4%)
  between operations  5 us (1%)
    psum x9, blocking collectives, one_axis_at_a_time(): shard = lax.psum(shard, axis)  159 us
    all_to_all x3, waiting for transfers between devices, from_everyone(): return lax.all_to_all(copies, axis, split_axis=0, concat_axis=0, tiled=True)  91.1 us
    all_to_all x3, waiting for transfers between devices, reduce_gradient(): lax.all_to_all(gradient, 'dp', split_axis=1, concat_axis=0, tiled=True)  81.3 us
    all_to_all x3, starting transfers between devices, reduce_gradient(): lax.all_to_all(gradient, 'dp', split_axis=1, concat_axis=0, tiled=True)  21.1 us
    unnamed x51, local copies, waits for them, and re-layouts  13 us
    unnamed x3, other arithmetic  12.8 us
    all_to_all x3, starting transfers between devices, from_everyone(): return lax.all_to_all(copies, axis, split_axis=0, concat_axis=0, tiled=True)  12.1 us
    all_to_all x1, blocking collectives, from_everyone(): return lax.all_to_all(copies, axis, split_axis=0, concat_axis=0, tiled=True)  9.54 us
  transfers between devices with their start and end apart: 6, of which 6 were waited for; matrix products, arithmetic and copies ran while one was open for 4% of the time, Pallas kernels for 0%

commit v1 on v0

v1 whole, which is shorter than its diff:
```python
import jax
import jax.numpy as jnp
from jax import lax
from jax.experimental import pallas as pl
from jax.experimental.pallas import tpu as pltpu
from jax.sharding import Mesh
from jax.sharding import PartitionSpec as P

MESH = pl.DeviceIdType.MESH
F32 = jnp.float32
BF16 = jnp.bfloat16

ROW = ("zhi", "x", "core")
ROW_DP = ("zhi", "x", "core", "dp")

tiny_square = 1e-30
decay_rate = 0.9
learn_rate = 0.01

N = 8
HEIGHTS = (32, 40, 32)
WIDTHS = (1280, 1024, 1024)
FULL_ROWS = (4096, 5120, 4096)
FULL_COLS = (5120, 4096, 4096)
BATCHES = ((0, 1), (2,))
LAYOUT = (((0, 0, 0, 8), (1, 1, 0, 8), (2, 0, 8, 10)), ((0, 2, 0, 8),))
Y_ROWS = (0, 32, 72)


def remote(src, dst, send_sem, recv_sem, device):
    return pltpu.make_async_remote_copy(
        src_ref=src, dst_ref=dst, send_sem=send_sem, recv_sem=recv_sem, device_id=device, device_id_type=MESH
    )


def to_column(row, height):
    sub = lax.broadcasted_iota(jnp.int32, (height, 128), 0)
    lane = lax.broadcasted_iota(jnp.int32, (height, 128), 1)
    return jnp.sum(jnp.where(sub == lane, jnp.broadcast_to(row, (height, 128)), 0.0), axis=1, keepdims=True)


def to_row(column, height):
    sub = lax.broadcasted_iota(jnp.int32, (height, 128), 0)
    lane = lax.broadcasted_iota(jnp.int32, (height, 128), 1)
    return jnp.sum(jnp.where(sub == lane, jnp.broadcast_to(column, (height, 128)), 0.0), axis=0, keepdims=True)


def kernel(*refs):
    grads, masters, rows, columns = refs[0:3], refs[3:6], refs[6:9], refs[9:12]
    updated, weights, rows_next, columns_next, steps = refs[12:15], refs[15:18], refs[18:21], refs[21:24], refs[24:27]
    (
        part0, part1, part2, raw0, raw1, raw2, acc0, acc1, acc2,
        rfac0, rfac1, rfac2,
        ysend, yrecv, piece, pieces_in, zsend, zrecv, total, fin, colstat,
        rs_send, rs_recv, ag_send, ag_recv, y_sems, p_sems, z_sems, f_sems,
    ) = refs[27:]
    parts, raws, accs, rfacs = (part0, part1, part2), (raw0, raw1, raw2), (acc0, acc1, acc2), (rfac0, rfac1, rfac2)

    k = lax.axis_index("dp")
    zhi, x, core, y = lax.axis_index("zhi"), lax.axis_index("x"), lax.axis_index("core"), lax.axis_index("col")
    p = x * 2 + core
    q = zhi * 8 + k
    n = y * 8 + p

    def z_peer(o):
        t = lax.rem(q + o, 16)
        return {"zhi": t // 8, "dp": lax.rem(t, 8)}

    def p_peer(t):
        return {"x": t // 2, "core": lax.rem(t, 2)}

    def plane_peer(o):
        t = lax.rem(n + o, 32)
        s = lax.rem(t, 8)
        return {"x": s // 2, "core": lax.rem(s, 2), "col": t // 8}

    barrier = pltpu.get_barrier_semaphore()

    @pl.loop(1, 16)
    def _(o):
        pl.semaphore_signal(barrier, inc=1, device_id=z_peer(o), device_id_type=MESH)

    @pl.loop(1, 32)
    def _(o):
        pl.semaphore_signal(barrier, inc=1, device_id=plane_peer(o), device_id_type=MESH)

    pl.semaphore_wait(barrier, 46)

    a = k // 4
    near = jnp.where(a == 0, k, 7 - k)
    far = 7 - near

    def real(jd, d):
        return jd + d * (7 - 2 * jd)

    def raw_copy(m, d, source, jd):
        j = real(jd, d)
        return remote(
            grads[m].at[j], raws[m].at[d, source, j], rs_send.at[m, d, j], rs_recv.at[m, source, d, j],
            {"dp": real(jnp.minimum(jd, 2), d)},
        )

    def part_copy(m, d, here, jd):
        j = real(jd, d)
        return remote(
            parts[m].at[d, j], parts[m].at[d, j], rs_send.at[m, d, j], rs_recv.at[m, 0, d, j],
            {"dp": real(jnp.minimum(here + 1, 7), d)},
        )

    def send_raw(m):
        @pl.when(near < 2)
        def _():
            @pl.loop(0, 7)
            def _(s):
                jd = 7 - s

                @pl.when(jd > near)
                def _():
                    raw_copy(m, a, near, jd).start()

    def forward_first(m, jd):
        j = real(jd, a)

        @pl.when((near == 2) & (jd > near))
        def _():
            raw_copy(m, a, 0, jd).wait_recv()
            raw_copy(m, a, 1, jd).wait_recv()
            parts[m][a, j] = raws[m][a, 0, j].astype(F32) + raws[m][a, 1, j].astype(F32) + grads[m][j].astype(F32)
            part_copy(m, a, near, jd).start()

        @pl.when((near == 3) & (jd > near))
        def _():
            forward_part(m, a, near, jd)

    def forward_part(m, d, here, jd):
        j = real(jd, d)
        part_copy(m, d, here, jd).wait_recv()
        parts[m][d, j] = parts[m][d, j] + grads[m][j].astype(F32)
        part_copy(m, d, here, jd).start()

    lag = jnp.where(near == 2, 5, jnp.where(near == 3, 2, 0))

    def reduce_chain(m):
        @pl.loop(0, 12)
        def _(u):
            @pl.when(u < 7)
            def _():
                forward_first(m, 7 - u)

            s = u - lag

            @pl.when((s >= 0) & (s < 7) & (7 - s > far))
            def _():
                forward_part(m, 1 - a, far, 7 - s)

    def own_block(m):
        b = 1 - a
        part_copy(m, b, far, far).wait_recv()
        accs[m][...] = parts[m][b, k] + grads[m][k].astype(F32)

        @pl.when((near == 1) | (near == 2))
        def _():
            raw_copy(m, a, 0, near).wait_recv()
            accs[m][...] = accs[m][...] + raws[m][a, 0, k].astype(F32)

        @pl.when(near == 2)
        def _():
            raw_copy(m, a, 1, near).wait_recv()
            accs[m][...] = accs[m][...] + raws[m][a, 1, k].astype(F32)

        @pl.when(near == 3)
        def _():
            part_copy(m, a, near, near).wait_recv()
            accs[m][...] = accs[m][...] + parts[m][a, k]

        accs[m][...] = accs[m][...] * 0.125

    def y_copy(b, o):
        lo = Y_ROWS[BATCHES[b][0]]
        size = sum(HEIGHTS[m] for m in BATCHES[b])
        t = lax.rem(y + o, 4)
        return remote(
            ysend.at[pl.ds(lo, size)], yrecv.at[o, pl.ds(lo, size)], y_sems.at[0, b, o], y_sems.at[1, b, o], {"col": t}
        )

    def stats_rows(b):
        for m in BATCHES[b]:
            square = accs[m][...] * accs[m][...] + tiny_square
            total_row = jnp.sum(square, axis=1, keepdims=True)
            ysend[pl.ds(Y_ROWS[m], HEIGHTS[m])] = jnp.broadcast_to(total_row, (HEIGHTS[m], 128))
        for o in range(1, 4):
            y_copy(b, o).start()

    def p_copy(b, o):
        t = lax.rem(p + o, 8)
        return remote(piece.at[b, t], pieces_in.at[b, o], p_sems.at[0, b, o], p_sems.at[1, b, o], p_peer(t))

    def stats_columns(b):
        for o in range(1, 4):
            y_copy(b, o).wait_recv()
        piece[b] = jnp.zeros((8, 8, 128), F32)
        for m in BATCHES[b]:
            height = HEIGHTS[m]
            at = pl.ds(Y_ROWS[m], height)
            across = (ysend[at] + yrecv[1, at]) + (yrecv[2, at] + yrecv[3, at])
            old = to_column(rows[m][...], height)
            new = decay_rate * old + (1.0 - decay_rate) * (across / FULL_COLS[m])
            rfacs[m][...] = new
            new_column = new[:, 0:1]
            rows_next[m][...] = to_row(new_column, height)
            row_sum = jnp.sum(new, axis=0, keepdims=True)
            g = accs[m][...]
            square = g * g
            plain = jnp.sum(square + tiny_square, axis=0, keepdims=True)
            weighted = jnp.sum(square * (1.0 / new_column), axis=0, keepdims=True)
            for slot, owner, lo, hi in LAYOUT[b]:
                if owner != m:
                    continue
                for group in range(lo, hi):
                    cut = slice(128 * group, 128 * group + 128)
                    piece[b, group - lo, 2 * slot : 2 * slot + 1] = plain[:, cut]
                    piece[b, group - lo, 2 * slot + 1 : 2 * slot + 2] = weighted[:, cut]
            at_row = 7 - BATCHES[b].index(m)
            for which in range(8):
                piece[b, which, at_row : at_row + 1] = row_sum
        for o in range(1, 8):
            p_copy(b, o).start()

    def z_copy(b, o):
        return remote(zsend.at[b], zrecv.at[b, o], z_sems.at[0, b, o], z_sems.at[1, b, o], z_peer(o))

    def stats_depth(b):
        tile = piece[b, p]
        for o in range(1, 8):
            p_copy(b, o).wait_recv()
            tile = tile + pieces_in[b, o]
        zsend[b] = tile

        @pl.loop(1, 16)
        def _(o):
            z_copy(b, o).start()

        colstat[b] = jnp.ones((8, 8, 128), F32)
        for slot, m, lo, hi in LAYOUT[b]:
            for group in range(lo, hi):
                cut = slice(128 * group, 128 * group + 128)
                colstat[b, group - lo, 2 * slot : 2 * slot + 1] = columns[m][:, cut]

    def f_copy(b, o):
        return remote(fin.at[b, n], fin.at[b, n], f_sems.at[0, b, o], f_sems.at[1, b, o], plane_peer(o))

    def next_column(old, total_square, m):
        return decay_rate * old + (1.0 - decay_rate) * (total_square / FULL_ROWS[m])

    def stats_plane(b):
        @pl.loop(1, 16)
        def _(o):
            z_copy(b, o).wait_recv()

        tile = zsend[b]
        for o in range(1, 16):
            tile = tile + zrecv[b, o]
        total[b] = tile
        fin[b, n] = tile
        for slot, m, lo, hi in LAYOUT[b]:
            plain = total[b, 2 * slot : 2 * slot + 1]
            weighted = total[b, 2 * slot + 1 : 2 * slot + 2]
            new = next_column(colstat[b, p, 2 * slot : 2 * slot + 1], plain, m)
            ratio = jnp.sum(weighted / new, axis=1, keepdims=True)
            fin[b, n, 2 * slot + 1 : 2 * slot + 2] = jnp.broadcast_to(ratio, (1, 128))

        @pl.loop(1, 32)
        def _(o):
            f_copy(b, o).start()

    def finish(b):
        @pl.loop(1, 32)
        def _(o):
            f_copy(b, o).wait_recv()

        everyone = fin[b, 0]
        for which in range(1, 32):
            everyone = everyone + fin[b, which]
        for m in BATCHES[b]:
            for slot, owner, lo, hi in LAYOUT[b]:
                if owner != m:
                    continue
                for group in range(lo, hi):
                    cut = slice(128 * group, 128 * group + 128)
                    plain = fin[b, y * 8 + (group - lo), 2 * slot : 2 * slot + 1]
                    columns_next[m][:, cut] = next_column(columns[m][:, cut], plain, m)
            at_row = 7 - BATCHES[b].index(m)
            row_mean = total[b, at_row : at_row + 1] / FULL_ROWS[m]
            ratio = sum(
                everyone[2 * slot + 1 : 2 * slot + 2] for slot, owner, _, _ in LAYOUT[b] if owner == m
            )
            mean_square = row_mean * ratio / (FULL_ROWS[m] * FULL_COLS[m])
            clip = jnp.maximum(1.0, jnp.sqrt(mean_square))
            row_scale = (jnp.sqrt(row_mean) / clip) / jnp.sqrt(rfacs[m][...])
            column_scale = 1.0 / jnp.sqrt(columns_next[m][...])
            step = accs[m][...] * row_scale[:, 0:1] * column_scale
            steps[m][...] = step
            new = masters[m][...] - learn_rate * step
            updated[m][...] = new
            weights[m][k] = new.astype(BF16)

    def w_copy(m, d, i):
        to = jnp.clip(k + 1 - 2 * d, 0, 7)
        return remote(weights[m].at[i], weights[m].at[i], ag_send.at[m, d, i], ag_recv.at[m, i], {"dp": to})

    def gather_start(m):
        for d in (0, 1):

            @pl.when(k != 7 * (1 - d))
            def _():
                w_copy(m, d, k).start()

    def gather_step(m, s):
        for d in (0, 1):
            i = k - s if d == 0 else k + s

            @pl.when((i >= 0) & (i <= 7))
            def _():
                w_copy(m, d, i).wait_recv()

                @pl.when(k != 7 * (1 - d))
                def _():
                    w_copy(m, d, i).start()

    for m in range(3):
        send_raw(m)
    for m in range(3):
        reduce_chain(m)
    for m in range(3):
        own_block(m)
    for b in (0, 1):
        stats_rows(b)
    for b in (0, 1):
        stats_columns(b)
    for b in (0, 1):
        stats_depth(b)
    for b in (0, 1):
        stats_plane(b)
    for b in (0, 1):
        finish(b)
    for m in range(3):
        gather_start(m)

    @pl.loop(1, 8)
    def _(s):
        for m in range(3):
            gather_step(m, s)

    @pl.loop(0, 8)
    def _(j):
        for m in range(3):

            @pl.when((near < 2) & (real(j, a) > near))
            def _():
                raw_copy(m, a, near, real(j, a)).wait_send()

            @pl.when((near >= 2) & (real(j, a) > near))
            def _():
                part_copy(m, a, near, real(j, a)).wait_send()

            @pl.when(real(j, 1 - a) > far)
            def _():
                part_copy(m, 1 - a, far, real(j, 1 - a)).wait_send()

            for d in (0, 1):
                held = (j <= k) if d == 0 else (j >= k)

                @pl.when(held & (k != 7 * (1 - d)))
                def _():
                    w_copy(m, d, j).wait_send()

    for b in (0, 1):
        for o in range(1, 4):
            y_copy(b, o).wait_send()
        for o in range(1, 8):
            p_copy(b, o).wait_send()

        @pl.loop(1, 16)
        def _(o):
            z_copy(b, o).wait_send()

        @pl.loop(1, 32)
        def _(o):
            f_copy(b, o).wait_send()


def body(*args):
    grads = [args[4 * m].reshape(N, HEIGHTS[m], WIDTHS[m]) for m in range(3)]
    masters = [args[4 * m + 1] for m in range(3)]
    rows = [jnp.pad(args[4 * m + 2], (0, 128 - HEIGHTS[m])).reshape(1, 128) for m in range(3)]
    columns = [args[4 * m + 3].reshape(1, WIDTHS[m]) for m in range(3)]
    shape = jax.ShapeDtypeStruct
    blocks = list(zip(HEIGHTS, WIDTHS))
    out_shape = (
        [shape(b, F32) for b in blocks]
        + [shape((N, *b), BF16) for b in blocks]
        + [shape((1, 128), F32)] * 3
        + [shape((1, w), F32) for w in WIDTHS]
        + [shape(b, F32) for b in blocks]
    )
    vmem = pl.BlockSpec(memory_space=pltpu.VMEM)
    dma = pltpu.SemaphoreType.DMA
    out = pl.pallas_call(
        kernel,
        out_shape=out_shape,
        in_specs=[vmem] * 12,
        out_specs=[vmem] * 15,
        scratch_shapes=(
            [pltpu.VMEM((2, N, *b), F32) for b in blocks]
            + [pltpu.VMEM((2, 2, N, *b), BF16) for b in blocks]
            + [pltpu.VMEM(b, F32) for b in blocks]
            + [pltpu.VMEM((h, 128), F32) for h in HEIGHTS]
            + [
                pltpu.VMEM((104, 128), F32),
                pltpu.VMEM((4, 104, 128), F32),
                pltpu.VMEM((2, 8, 8, 128), F32),
                pltpu.VMEM((2, 8, 8, 128), F32),
                pltpu.VMEM((2, 8, 128), F32),
                pltpu.VMEM((2, 16, 8, 128), F32),
                pltpu.VMEM((2, 8, 128), F32),
                pltpu.VMEM((2, 32, 8, 128), F32),
                pltpu.VMEM((2, 8, 8, 128), F32),
                dma((3, 2, 8)),
                dma((3, 2, 2, 8)),
                dma((3, 2, 8)),
                dma((3, 8)),
                dma((2, 2, 4)),
                dma((2, 2, 8)),
                dma((2, 2, 16)),
                dma((2, 2, 32)),
            ]
        ),
        compiler_params=pltpu.CompilerParams(
            collective_id=0, has_side_effects=True, vmem_limit_bytes=60 * 1024 * 1024
        ),
    )(*grads, *masters, *rows, *columns)
    result = []
    for m in range(3):
        result += [
            out[m],
            out[3 + m].reshape(N * HEIGHTS[m], WIDTHS[m]),
            out[6 + m][0, : HEIGHTS[m]],
            out[9 + m].reshape(WIDTHS[m]),
            out[12 + m],
        ]
    return tuple(result)


def solution(mesh):
    finer = Mesh(mesh.devices.reshape(mesh.shape["dp"], 2, 4, 2, mesh.shape["col"]), ("dp", *ROW, "col"))
    one = (P("dp", ROW, "col"), P(ROW_DP, "col"), P(ROW_DP), P("col"))
    back = (P(ROW_DP, "col"), P(ROW, "col"), P(ROW_DP), P("col"), P(ROW_DP, "col"))
    return jax.shard_map(body, mesh=finer, in_specs=one * 3, out_specs=back * 3, check_vma=False)
```

time: 417 us -> 193 us (0.46)
  Pallas kernels: 0 us -> 174 us
  waiting for transfers between devices: 172 us -> 0 us
  blocking collectives: 168 us -> 0 us
  starting transfers between devices: 33.2 us -> 0 us
  other arithmetic: 19.8 us -> 0.62 us
  between operations: 5 us -> 0.7 us
    pallas_call x0 -> x1, Pallas kernels: none -> 174 us  [body(): pl.pallas_call(kernel, out_shape=out_shape, in_specs=[vmem] * 12, out_spe...]
    all_to_all x6 -> x0, waiting for transfers between devices: 172 us -> none  [the longest x3 91.1 us: from_everyone(): return lax.all_to_all(copies, axis, split_axis=0, concat_axis=0, tiled=True)]
    psum x9 -> x0, blocking collectives: 159 us -> none  [one_axis_at_a_time(): shard = lax.psum(shard, axis)]
    all_to_all x6 -> x0, starting transfers between devices: 33.2 us -> none  [the longest x3 21.1 us: reduce_gradient(): lax.all_to_all(gradient, 'dp', split_axis=1, concat_axis=0, tiled=True)]
    unnamed x3 -> x0, other arithmetic: 12.8 us -> none
    all_to_all x1 -> x0, blocking collectives: 9.54 us -> none  [from_everyone(): return lax.all_to_all(copies, axis, split_axis=0, concat_axis=0, tiled=True)]
    reduce_sum x12 -> x0, other arithmetic: 4.28 us -> none  [the longest x1 0.76 us: body(): jnp.sum(raws[1] * raws[1])]
    unnamed x51 -> x43, local copies, waits for them, and re-layouts: 13 us -> 12.4 us
  transfers between devices with their start and end apart: 6 -> 0, of which waited for: 6 -> 0; matrix products, arithmetic and copies ran while one was open for 4% -> 0% of each run, Pallas kernels for 0% -> 0%
where the time goes in v1:
time: 193 us; the launch traced here: 192 us
  Pallas kernels  174 us (90%)
  local copies, waits for them, and re-layouts  16.2 us (8%)
    pallas_call x1, Pallas kernels, body(): pl.pallas_call(kernel, out_shape=out_shape, in_specs=[vmem] * 12, out_spe...  174 us
    unnamed x43, local copies, waits for them, and re-layouts  12.4 us

profile of v1, /device:TPU:6, one launch (start us, length us, event | category | flops | bytes accessed | tf_op | source)
XLA Modules:
  0.0 192.0 jit_solution(2430351091792464523)
XLA Ops:
  0.6 0.0 copy-start.12
  0.7 1.3 reshape.81.refs_9_
  2.0 0.0 copy-done.12
  2.0 0.5 pad_bitcast_fusion.refs_8_
  2.5 0.1 copy-done.13
  2.6 0.5 pad_bitcast_fusion.1.refs_7_
  3.1 0.1 copy-done.14
  3.3 0.5 pad_bitcast_fusion.2.refs_6_
  3.8 174.4 %shard_map.235 = (f32[32,1280]{1,0:T(8,128)}, f32[40,1024]{1,0:T(8,128)}, f32[32,1024]{1,0:T(8,128)}, bf16[8,32,1280]{2,1,0:T(8,128)(2,1)}, bf16[8,40,1024]{2,1,...) custom-call(bf16[8,32,1280]{2,1,0:T(8,128)(2,1)} %bitcast.24, ...), custom_call_target="tpu_custom_call" | custom-call | tf_op jit(solution)/shard_map/pallas_call | solution.py:408
  178.2 0.0 copy-start.10
  178.2 0.0 copy-start.11
  178.2 0.7 copy-done.10
  178.9 0.0 copy-done.11
  178.9 0.5 slice_bitcast_fusion
  179.4 0.7 copy-done.7
  180.1 0.6 reduce
  180.7 0.6 copy-done.15
  181.3 0.5 slice_bitcast_fusion.1
  181.9 1.6 copy.38
  183.4 2.0 %copy.39 = bf16[256,1280]{1,0:T(8,128)(2,1)} copy(bf16[256,1280]{1,0:T(8,128)(2,1)} %bitcast.23) | data formatting | bytes 1310720
  185.5 0.0 copy-done.4
  185.5 0.7 copy.40
  186.2 0.3 copy-done.3
  186.5 0.7 copy.41
  187.1 0.0 copy-done
  187.1 0.8 copy.42
  188.0 0.6 copy.43
  188.6 0.7 copy.44
  189.3 0.7 copy.45
  189.9 0.8 copy.46
  190.7 0.6 copy.47
  191.3 0.7 copy.48
  (19 shorter events, 0.0 us)
Async XLA Ops:
  0.6 1.3 copy-start.12
  2.0 0.7 copy-start.13
  2.6 0.7 copy-start.14
  178.2 0.7 copy-start.10
  178.2 0.7 copy-start.11
  179.4 0.7 copy-start.7
  180.7 0.6 copy-start.15
  183.4 2.0 %copy-start.4 = (f32[32,1280]{1,0:T(8,128)S(1)}, f32[32,1280]{1,0:T(8,128)}, u32[]{:S(2)}) copy-start(f32[32,1280]{1,0:T(8,128)} %get-tuple-element.66) | copy-start | bytes 491524
  183.4 3.7 %copy-start = (bf16[8,40,1024]{2,1,0:T(8,128)(2,1)S(1)}, bf16[8,40,1024]{2,1,0:T(8,128)(2,1)}, u32[]{:S(2)}) copy-start(bf16[8,40,1024]{2,1,0:T(8,128)(2,1)} %get-tuple-element.36) | copy-start | bytes 1966084
  185.5 1.0 copy-start.3
  187.1 0.9 copy-start.9
  187.1 1.4 copy-start.2
  187.1 2.1 %copy-start.6 = (f32[32,1024]{1,0:T(8,128)S(1)}, f32[32,1024]{1,0:T(8,128)}, u32[]{:S(2)}) copy-start(f32[32,1024]{1,0:T(8,128)} %get-tuple-element.72) | copy-start | bytes 393220
  188.0 1.9 %copy-start.1 = (bf16[8,32,1024]{2,1,0:T(8,128)(2,1)S(1)}, bf16[8,32,1024]{2,1,0:T(8,128)(2,1)}, u32[]{:S(2)}) copy-start(bf16[8,32,1024]{2,1,0:T(8,128)(2,1)} %get-tuple-element.41) | copy-start | bytes 1572868
  189.9 0.8 copy-start.8
  189.9 1.4 copy-start.5

commit v2 on v1

--- a/solution.py
+++ b/solution.py
@@ -22,9 +22,8 @@
 WIDTHS = (1280, 1024, 1024)
 FULL_ROWS = (4096, 5120, 4096)
 FULL_COLS = (5120, 4096, 4096)
-BATCHES = ((0, 1), (2,))
-LAYOUT = (((0, 0, 0, 8), (1, 1, 0, 8), (2, 0, 8, 10)), ((0, 2, 0, 8),))
-Y_ROWS = (0, 32, 72)
+BATCHES = ((0,), (1, 2))
+LAYOUT = (((0, 0, 0, 8), (1, 0, 8, 10)), ((0, 1, 0, 8), (1, 2, 0, 8)))
 
 
 def remote(src, dst, send_sem, recv_sem, device):
@@ -93,101 +92,88 @@
     def real(jd, d):
         return jd + d * (7 - 2 * jd)
 
-    def raw_copy(m, d, source, jd):
+    def half(m, c):
+        return pl.ds(c * (WIDTHS[m] // 2), WIDTHS[m] // 2)
+
+    def raw_copy(m, jd, c):
+        j = real(jd, a)
+        return remote(
+            grads[m].at[j, :, half(m, c)], raws[m].at[a, j, :, half(m, c)], rs_send.at[m, a, j, c],
+            rs_recv.at[m, a, j, c], {"dp": real(1, a)},
+        )
+
+    def part_copy(m, d, here, jd, c):
         j = real(jd, d)
+        block = parts[m].at[d, j, :, half(m, c)]
         return remote(
-            grads[m].at[j], raws[m].at[d, source, j], rs_send.at[m, d, j], rs_recv.at[m, source, d, j],
-            {"dp": real(jnp.minimum(jd, 2), d)},
+            block, block, rs_send.at[m, d, j, c], rs_recv.at[m, d, j, c], {"dp": real(jnp.minimum(here + 1, 7), d)}
         )
 
-    def part_copy(m, d, here, jd):
-        j = real(jd, d)
-        return remote(
-            parts[m].at[d, j], parts[m].at[d, j], rs_send.at[m, d, j], rs_recv.at[m, 0, d, j],
-            {"dp": real(jnp.minimum(here + 1, 7), d)},
-        )
-
     def send_raw(m):
-        @pl.when(near < 2)
+        @pl.when(near == 0)
         def _():
             @pl.loop(0, 7)
             def _(s):
-                jd = 7 - s
-
-                @pl.when(jd > near)
-                def _():
-                    raw_copy(m, a, near, jd).start()
+                for c in (0, 1):
+                    raw_copy(m, 7 - s, c).start()
 
     def forward_first(m, jd):
         j = real(jd, a)
 
-        @pl.when((near == 2) & (jd > near))
-        def _():
-            raw_copy(m, a, 0, jd).wait_recv()
-            raw_copy(m, a, 1, jd).wait_recv()
-            parts[m][a, j] = raws[m][a, 0, j].astype(F32) + raws[m][a, 1, j].astype(F32) + grads[m][j].astype(F32)
-            part_copy(m, a, near, jd).start()
-
-        @pl.when((near == 3) & (jd > near))
+        @pl.when((near == 1) & (jd > near))
+        def _():
+            for c in (0, 1):
+                cut = half(m, c)
+                raw_copy(m, jd, c).wait_recv()
+                parts[m][a, j, :, cut] = raws[m][a, j, :, cut].astype(F32) + grads[m][j, :, cut].astype(F32)
+                part_copy(m, a, near, jd, c).start()
+
+        @pl.when((near >= 2) & (jd > near))
         def _():
             forward_part(m, a, near, jd)
 
     def forward_part(m, d, here, jd):
         j = real(jd, d)
-        part_copy(m, d, here, jd).wait_recv()
-        parts[m][d, j] = parts[m][d, j] + grads[m][j].astype(F32)
-        part_copy(m, d, here, jd).start()
-
-    lag = jnp.where(near == 2, 5, jnp.where(near == 3, 2, 0))
-
-    def reduce_chain(m):
-        @pl.loop(0, 12)
-        def _(u):
-            @pl.when(u < 7)
-            def _():
-                forward_first(m, 7 - u)
-
-            s = u - lag
-
-            @pl.when((s >= 0) & (s < 7) & (7 - s > far))
-            def _():
-                forward_part(m, 1 - a, far, 7 - s)
+        for c in (0, 1):
+            cut = half(m, c)
+            part_copy(m, d, here, jd, c).wait_recv()
+            parts[m][d, j, :, cut] = parts[m][d, j, :, cut] + grads[m][j, :, cut].astype(F32)
+            part_copy(m, d, here, jd, c).start()
+
+    def forward_second(m, r):
+        @pl.when((r >= 0) & (7 - r > far))
+        def _():
+            forward_part(m, 1 - a, far, 7 - r)
 
     def own_block(m):
         b = 1 - a
-        part_copy(m, b, far, far).wait_recv()
+        for c in (0, 1):
+            part_copy(m, b, far, far, c).wait_recv()
         accs[m][...] = parts[m][b, k] + grads[m][k].astype(F32)
 
-        @pl.when((near == 1) | (near == 2))
-        def _():
-            raw_copy(m, a, 0, near).wait_recv()
-            accs[m][...] = accs[m][...] + raws[m][a, 0, k].astype(F32)
-
-        @pl.when(near == 2)
-        def _():
-            raw_copy(m, a, 1, near).wait_recv()
-            accs[m][...] = accs[m][...] + raws[m][a, 1, k].astype(F32)
-
-        @pl.when(near == 3)
-        def _():
-            part_copy(m, a, near, near).wait_recv()
+        @pl.when(near == 1)
+        def _():
+            for c in (0, 1):
+                raw_copy(m, near, c).wait_recv()
+            accs[m][...] = accs[m][...] + raws[m][a, k].astype(F32)
+
+        @pl.when(near >= 2)
+        def _():
+            for c in (0, 1):
+                part_copy(m, a, near, near, c).wait_recv()
             accs[m][...] = accs[m][...] + parts[m][a, k]
 
         accs[m][...] = accs[m][...] * 0.125
 
     def y_copy(b, o):
-        lo = Y_ROWS[BATCHES[b][0]]
-        size = sum(HEIGHTS[m] for m in BATCHES[b])
         t = lax.rem(y + o, 4)
-        return remote(
-            ysend.at[pl.ds(lo, size)], yrecv.at[o, pl.ds(lo, size)], y_sems.at[0, b, o], y_sems.at[1, b, o], {"col": t}
-        )
+        return remote(ysend.at[b], yrecv.at[b, o], y_sems.at[0, b, o], y_sems.at[1, b, o], {"col": t})
 
     def stats_rows(b):
-        for m in BATCHES[b]:
+        for at_row, m in enumerate(BATCHES[b]):
             square = accs[m][...] * accs[m][...] + tiny_square
             total_row = jnp.sum(square, axis=1, keepdims=True)
-            ysend[pl.ds(Y_ROWS[m], HEIGHTS[m])] = jnp.broadcast_to(total_row, (HEIGHTS[m], 128))
+            ysend[b, at_row : at_row + 1] = to_row(total_row, HEIGHTS[m])
         for o in range(1, 4):
             y_copy(b, o).start()
 
@@ -201,14 +187,13 @@
         piece[b] = jnp.zeros((8, 8, 128), F32)
         for m in BATCHES[b]:
             height = HEIGHTS[m]
-            at = pl.ds(Y_ROWS[m], height)
-            across = (ysend[at] + yrecv[1, at]) + (yrecv[2, at] + yrecv[3, at])
-            old = to_column(rows[m][...], height)
-            new = decay_rate * old + (1.0 - decay_rate) * (across / FULL_COLS[m])
-            rfacs[m][...] = new
-            new_column = new[:, 0:1]
-            rows_next[m][...] = to_row(new_column, height)
-            row_sum = jnp.sum(new, axis=0, keepdims=True)
+            at = slice(BATCHES[b].index(m), BATCHES[b].index(m) + 1)
+            across = (ysend[b, at] + yrecv[b, 1, at]) + (yrecv[b, 2, at] + yrecv[b, 3, at])
+            new = decay_rate * rows[m][...] + (1.0 - decay_rate) * (across / FULL_COLS[m])
+            rows_next[m][...] = new
+            new_column = to_column(new, height)
+            rfacs[m][...] = jnp.broadcast_to(new_column, (height, 128))
+            row_sum = jnp.broadcast_to(jnp.sum(new_column, axis=0, keepdims=True), (1, 128))
             g = accs[m][...]
             square = g * g
             plain = jnp.sum(square + tiny_square, axis=0, keepdims=True)
@@ -329,43 +314,85 @@
 
     for m in range(3):
         send_raw(m)
-    for m in range(3):
-        reduce_chain(m)
-    for m in range(3):
+
+    lag = jnp.where(near == 1, 6, jnp.where(near == 2, 4, 2))
+    lag_pair = jnp.where(near == 1, 4, jnp.where(near == 2, 2, 1))
+
+    @pl.loop(0, 7)
+    def _(u):
+        forward_first(0, 7 - u)
+        forward_second(0, u - lag)
+
+    @pl.loop(0, 7)
+    def _(u):
+        for m in (1, 2):
+            forward_first(m, 7 - u)
+        for m in (1, 2):
+            forward_second(m, u - lag_pair)
+
+        @pl.when(u == 0)
+        def _():
+            own_block(0)
+            stats_rows(0)
+
+        @pl.when(u == 1)
+        def _():
+            stats_columns(0)
+
+        @pl.when(u == 2)
+        def _():
+            stats_depth(0)
+
+        @pl.when(u == 5)
+        def _():
+            stats_plane(0)
+
+    for m in (1, 2):
         own_block(m)
-    for b in (0, 1):
-        stats_rows(b)
-    for b in (0, 1):
-        stats_columns(b)
-    for b in (0, 1):
-        stats_depth(b)
-    for b in (0, 1):
-        stats_plane(b)
-    for b in (0, 1):
-        finish(b)
-    for m in range(3):
+    stats_rows(1)
+    finish(0)
+    gather_start(0)
+    stats_columns(1)
+    gather_step(0, 1)
+    stats_depth(1)
+    gather_step(0, 2)
+    gather_step(0, 3)
+    stats_plane(1)
+    gather_step(0, 4)
+    finish(1)
+    for m in (1, 2):
         gather_start(m)
-
-    @pl.loop(1, 8)
+    gather_step(0, 5)
+    for m in (1, 2):
+        gather_step(m, 1)
+    gather_step(0, 6)
+    for m in (1, 2):
+        gather_step(m, 2)
+    gather_step(0, 7)
+
+    @pl.loop(3, 8)
     def _(s):
-        for m in range(3):
+        for m in (1, 2):
             gather_step(m, s)
 
     @pl.loop(0, 8)
     def _(j):
         for m in range(3):
 
-            @pl.when((near < 2) & (real(j, a) > near))
+            @pl.when((near == 0) & (real(j, a) > 0))
             def _():
-                raw_copy(m, a, near, real(j, a)).wait_send()
-
-            @pl.when((near >= 2) & (real(j, a) > near))
+                for c in (0, 1):
+                    raw_copy(m, real(j, a), c).wait_send()
+
+            @pl.when((near >= 1) & (real(j, a) > near))
             def _():
-                part_copy(m, a, near, real(j, a)).wait_send()
+                for c in (0, 1):
+                    part_copy(m, a, near, real(j, a), c).wait_send()
 
             @pl.when(real(j, 1 - a) > far)
             def _():
-                part_copy(m, 1 - a, far, real(j, 1 - a)).wait_send()
+                for c in (0, 1):
+                    part_copy(m, 1 - a, far, real(j, 1 - a), c).wait_send()
 
             for d in (0, 1):
                 held = (j <= k) if d == 0 else (j >= k)
@@ -412,12 +439,12 @@
         out_specs=[vmem] * 15,
         scratch_shapes=(
             [pltpu.VMEM((2, N, *b), F32) for b in blocks]
-            + [pltpu.VMEM((2, 2, N, *b), BF16) for b in blocks]
+            + [pltpu.VMEM((2, N, *b), BF16) for b in blocks]
             + [pltpu.VMEM(b, F32) for b in blocks]
             + [pltpu.VMEM((h, 128), F32) for h in HEIGHTS]
             + [
-                pltpu.VMEM((104, 128), F32),
-                pltpu.VMEM((4, 104, 128), F32),
+                pltpu.VMEM((2, 8, 128), F32),
+                pltpu.VMEM((2, 4, 8, 128), F32),
                 pltpu.VMEM((2, 8, 8, 128), F32),
                 pltpu.VMEM((2, 8, 8, 128), F32),
                 pltpu.VMEM((2, 8, 128), F32),
@@ -425,8 +452,8 @@
                 pltpu.VMEM((2, 8, 128), F32),
                 pltpu.VMEM((2, 32, 8, 128), F32),
                 pltpu.VMEM((2, 8, 8, 128), F32),
-                dma((3, 2, 8)),
-                dma((3, 2, 2, 8)),
+                dma((3, 2, 8, 2)),
+                dma((3, 2, 8, 2)),
                 dma((3, 2, 8)),
                 dma((3, 8)),
                 dma((2, 2, 4)),

time: 193 us -> 165 us (0.85)
  Pallas kernels: 174 us -> 147 us
    pallas_call x1, Pallas kernels: 174 us -> 147 us  [body(): pl.pallas_call(kernel, out_shape=out_shape, in_specs=[vmem] * 12, out_spe...]
where the time goes in v2:
time: 165 us
  Pallas kernels  147 us (89%)
  local copies, waits for them, and re-layouts  16.2 us (10%)
    pallas_call x1, Pallas kernels, body(): pl.pallas_call(kernel, out_shape=out_shape, in_specs=[vmem] * 12, out_spe...  147 us
    unnamed x43, local copies, waits for them, and re-layouts  12.4 us

profile of v2, /device:TPU:6, one launch (start us, length us, event | category | flops | bytes accessed | tf_op | source)
XLA Modules:
  0.0 164.5 jit_solution(8294673791564444928)
XLA Ops:
  0.6 0.0 copy-start.12
  0.7 1.3 reshape.81.refs_9_
  2.0 0.0 copy-done.12
  2.0 0.5 pad_bitcast_fusion.refs_8_
  2.5 0.1 copy-done.13
  2.6 0.5 pad_bitcast_fusion.1.refs_7_
  3.1 0.1 copy-done.14
  3.3 0.5 pad_bitcast_fusion.2.refs_6_
  3.8 147.0 %shard_map.235 = (f32[32,1280]{1,0:T(8,128)}, f32[40,1024]{1,0:T(8,128)}, f32[32,1024]{1,0:T(8,128)}, bf16[8,32,1280]{2,1,0:T(8,128)(2,1)}, bf16[8,40,1024]{2,1,...) custom-call(bf16[8,32,1280]{2,1,0:T(8,128)(2,1)} %bitcast.24, ...), custom_call_target="tpu_custom_call" | custom-call | tf_op jit(solution)/shard_map/pallas_call | solution.py:435
  150.8 0.0 copy-start.10
  150.8 0.0 copy-start.11
  150.8 0.7 copy-done.10
  151.4 0.0 copy-done.11
  151.4 0.5 slice_bitcast_fusion
  152.0 0.7 copy-done.7
  152.7 0.6 reduce
  153.3 0.6 copy-done.15
  153.9 0.5 slice_bitcast_fusion.1
  154.4 1.6 copy.38
  156.0 2.0 %copy.39 = bf16[256,1280]{1,0:T(8,128)(2,1)} copy(bf16[256,1280]{1,0:T(8,128)(2,1)} %bitcast.23) | data formatting | bytes 1310720
  158.0 0.0 copy-done.4
  158.0 0.7 copy.40
  158.7 0.3 copy-done.3
  159.0 0.7 copy.41
  159.7 0.8 copy.42
  160.5 0.0 copy-done.9
  160.5 0.6 copy.43
  161.1 0.7 copy.44
  161.8 0.7 copy.45
  162.5 0.8 copy.46
  163.3 0.6 copy.47
  163.9 0.7 copy.48
  (19 shorter events, 0.0 us)
Async XLA Ops:
  0.6 1.3 copy-start.12
  2.0 0.7 copy-start.13
  2.6 0.7 copy-start.14
  150.8 0.7 copy-start.10
  150.8 0.7 copy-start.11
  152.0 0.7 copy-start.7
  153.3 0.6 copy-start.15
  156.0 2.0 %copy-start.4 = (f32[32,1280]{1,0:T(8,128)S(1)}, f32[32,1280]{1,0:T(8,128)}, u32[]{:S(2)}) copy-start(f32[32,1280]{1,0:T(8,128)} %get-tuple-element.66) | copy-start | bytes 491524
  156.0 3.7 %copy-start = (bf16[8,40,1024]{2,1,0:T(8,128)(2,1)S(1)}, bf16[8,40,1024]{2,1,0:T(8,128)(2,1)}, u32[]{:S(2)}) copy-start(bf16[8,40,1024]{2,1,0:T(8,128)(2,1)} %get-tuple-element.36) | copy-start | bytes 1966084
  158.0 1.0 copy-start.3
  159.7 0.9 copy-start.9
  159.7 1.4 copy-start.2
  159.7 2.1 %copy-start.6 = (f32[32,1024]{1,0:T(8,128)S(1)}, f32[32,1024]{1,0:T(8,128)}, u32[]{:S(2)}) copy-start(f32[32,1024]{1,0:T(8,128)} %get-tuple-element.72) | copy-start | bytes 393220
  160.5 1.9 %copy-start.1 = (bf16[8,32,1024]{2,1,0:T(8,128)(2,1)S(1)}, bf16[8,32,1024]{2,1,0:T(8,128)(2,1)}, u32[]{:S(2)}) copy-start(bf16[8,32,1024]{2,1,0:T(8,128)(2,1)} %get-tuple-element.41) | copy-start | bytes 1572868
  162.5 0.8 copy-start.8
  162.5 1.4 copy-start.5

commit v3 on v2

--- a/solution.py
+++ b/solution.py
@@ -44,15 +44,24 @@
     return jnp.sum(jnp.where(sub == lane, jnp.broadcast_to(column, (height, 128)), 0.0), axis=0, keepdims=True)
 
 
+def as_row(ref, height):
+    return jnp.pad(ref[...].reshape(1, height), ((0, 0), (0, 128 - height)))
+
+
 def kernel(*refs):
-    grads, masters, rows, columns = refs[0:3], refs[3:6], refs[6:9], refs[9:12]
+    given = refs[0:12]
     updated, weights, rows_next, columns_next, steps = refs[12:15], refs[15:18], refs[18:21], refs[21:24], refs[24:27]
     (
         part0, part1, part2, raw0, raw1, raw2, acc0, acc1, acc2,
         rfac0, rfac1, rfac2,
         ysend, yrecv, piece, pieces_in, zsend, zrecv, total, fin, colstat,
         rs_send, rs_recv, ag_send, ag_recv, y_sems, p_sems, z_sems, f_sems,
+        *held, load_sems,
     ) = refs[27:]
+    grads, masters, rows, columns = held[0:3], held[3:6], held[6:9], held[9:12]
+    loads = [pltpu.make_async_copy(given[i], held[i], load_sems.at[i]) for i in range(12)]
+    for load in loads:
+        load.start()
     parts, raws, accs, rfacs = (part0, part1, part2), (raw0, raw1, raw2), (acc0, acc1, acc2), (rfac0, rfac1, rfac2)
 
     k = lax.axis_index("dp")
@@ -83,6 +92,8 @@
     def _(o):
         pl.semaphore_signal(barrier, inc=1, device_id=plane_peer(o), device_id_type=MESH)
 
+    for load in loads:
+        load.wait()
     pl.semaphore_wait(barrier, 46)
 
     a = k // 4
@@ -189,7 +200,7 @@
             height = HEIGHTS[m]
             at = slice(BATCHES[b].index(m), BATCHES[b].index(m) + 1)
             across = (ysend[b, at] + yrecv[b, 1, at]) + (yrecv[b, 2, at] + yrecv[b, 3, at])
-            new = decay_rate * rows[m][...] + (1.0 - decay_rate) * (across / FULL_COLS[m])
+            new = decay_rate * as_row(rows[m], height) + (1.0 - decay_rate) * (across / FULL_COLS[m])
             rows_next[m][...] = new
             new_column = to_column(new, height)
             rfacs[m][...] = jnp.broadcast_to(new_column, (height, 128))
@@ -229,7 +240,7 @@
         for slot, m, lo, hi in LAYOUT[b]:
             for group in range(lo, hi):
                 cut = slice(128 * group, 128 * group + 128)
-                colstat[b, group - lo, 2 * slot : 2 * slot + 1] = columns[m][:, cut]
+                colstat[b, group - lo, 2 * slot : 2 * slot + 1] = columns[m][cut].reshape(1, 128)
 
     def f_copy(b, o):
         return remote(fin.at[b, n], fin.at[b, n], f_sems.at[0, b, o], f_sems.at[1, b, o], plane_peer(o))
@@ -273,7 +284,7 @@
                 for group in range(lo, hi):
                     cut = slice(128 * group, 128 * group + 128)
                     plain = fin[b, y * 8 + (group - lo), 2 * slot : 2 * slot + 1]
-                    columns_next[m][:, cut] = next_column(columns[m][:, cut], plain, m)
+                    columns_next[m][:, cut] = next_column(columns[m][cut].reshape(1, 128), plain, m)
             at_row = 7 - BATCHES[b].index(m)
             row_mean = total[b, at_row : at_row + 1] / FULL_ROWS[m]
             ratio = sum(
@@ -416,11 +427,22 @@
             f_copy(b, o).wait_send()
 
 
+def results_kernel(*refs):
+    copies = [pltpu.make_async_copy(refs[i], refs[15 + i], refs[30].at[i]) for i in range(9)]
+    for copy in copies:
+        copy.start()
+    for m in range(3):
+        refs[24 + m][...] = refs[9 + m][0, 0 : HEIGHTS[m]]
+        refs[27 + m][...] = refs[12 + m][0, :]
+    for copy in copies:
+        copy.wait()
+
+
 def body(*args):
     grads = [args[4 * m].reshape(N, HEIGHTS[m], WIDTHS[m]) for m in range(3)]
     masters = [args[4 * m + 1] for m in range(3)]
-    rows = [jnp.pad(args[4 * m + 2], (0, 128 - HEIGHTS[m])).reshape(1, 128) for m in range(3)]
-    columns = [args[4 * m + 3].reshape(1, WIDTHS[m]) for m in range(3)]
+    rows = [args[4 * m + 2] for m in range(3)]
+    columns = [args[4 * m + 3] for m in range(3)]
     shape = jax.ShapeDtypeStruct
     blocks = list(zip(HEIGHTS, WIDTHS))
     out_shape = (
@@ -435,7 +457,7 @@
     out = pl.pallas_call(
         kernel,
         out_shape=out_shape,
-        in_specs=[vmem] * 12,
+        in_specs=[pl.BlockSpec(memory_space=pltpu.HBM)] * 12,
         out_specs=[vmem] * 15,
         scratch_shapes=(
             [pltpu.VMEM((2, N, *b), F32) for b in blocks]
@@ -461,20 +483,36 @@
                 dma((2, 2, 16)),
                 dma((2, 2, 32)),
             ]
+            + [pltpu.VMEM((N, *b), BF16) for b in blocks]
+            + [pltpu.VMEM(b, F32) for b in blocks]
+            + [pltpu.VMEM((h,), F32) for h in HEIGHTS]
+            + [pltpu.VMEM((w,), F32) for w in WIDTHS]
+            + [dma((12,))]
         ),
         compiler_params=pltpu.CompilerParams(
-            collective_id=0, has_side_effects=True, vmem_limit_bytes=60 * 1024 * 1024
+            collective_id=0, has_side_effects=True, vmem_limit_bytes=28 * 1024 * 1024
         ),
-    )(*grads, *masters, *rows, *columns)
+    )(*[pltpu.with_memory_space_constraint(v, pltpu.HBM) for v in (*grads, *masters, *rows, *columns)])
+    anywhere = pl.BlockSpec(memory_space=pl.ANY)
+    final_shape = (
+        [shape(b, F32) for b in blocks]
+        + [shape((N, *b), BF16) for b in blocks]
+        + [shape(b, F32) for b in blocks]
+        + [shape((h,), F32) for h in HEIGHTS]
+        + [shape((w,), F32) for w in WIDTHS]
+    )
+    big = list(out[0:6]) + list(out[12:15])
+    final = pl.pallas_call(
+        results_kernel,
+        out_shape=final_shape,
+        in_specs=[vmem] * 15,
+        out_specs=[anywhere] * 9 + [vmem] * 6,
+        scratch_shapes=[dma((9,))],
+        compiler_params=pltpu.CompilerParams(vmem_limit_bytes=8 * 1024 * 1024),
+    )(*big, *out[6:12])
     result = []
     for m in range(3):
-        result += [
-            out[m],
-            out[3 + m].reshape(N * HEIGHTS[m], WIDTHS[m]),
-            out[6 + m][0, : HEIGHTS[m]],
-            out[9 + m].reshape(WIDTHS[m]),
-            out[12 + m],
-        ]
+        result += [final[m], final[3 + m].reshape(N * HEIGHTS[m], WIDTHS[m]), final[9 + m], final[12 + m], final[6 + m]]
     return tuple(result)
 
 

time: 165 us -> 147 us (0.89)
  local copies, waits for them, and re-layouts: 16.2 us -> 0 us
    unnamed x43 -> x0, local copies, waits for them, and re-layouts: 12.4 us -> none
    reshape x4 -> x0, local copies, waits for them, and re-layouts: 2.84 us -> none  [the longest x3 1.54 us: body(): jnp.pad(args[4 * m + 2], (0, 128 - HEIGHTS[m])).reshape(1, 128)]
    pallas_call x1 -> x2, Pallas kernels: 147 us -> 146 us  [the longest x1 144 us: body(): pl.pallas_call(kernel, out_shape=out_shape, in_specs=[pl.BlockSpec(memory...]
where the time goes in v3:
time: 147 us
  Pallas kernels  146 us (99%)
    pallas_call x1, Pallas kernels, body(): pl.pallas_call(kernel, out_shape=out_shape, in_specs=[pl.BlockSpec(memory...  144 us

profile of v3, /device:TPU:6, one launch (start us, length us, event | category | flops | bytes accessed | tf_op | source)
XLA Modules:
  0.0 147.1 jit_solution(5329524749869060472)
XLA Ops:
  0.7 144.2 %shard_map.235 = (f32[32,1280]{1,0:T(8,128)S(1)}, f32[40,1024]{1,0:T(8,128)S(1)}, f32[32,1024]{1,0:T(8,128)S(1)}, bf16[8,32,1280]{2,1,0:T(8,128)(2,1)S(1)}, bf16...) custom-call(bf16[8,32,1280]{2,1,0:T(8,128)(2,1)} %bitcast.6, ...), custom_call_target="tpu_custom_call" | custom-call | tf_op jit(solution)/shard_map/pallas_call | solution.py:457
  144.8 2.3 %shard_map.236 = (f32[32,1280]{1,0:T(8,128)}, f32[40,1024]{1,0:T(8,128)}, f32[32,1024]{1,0:T(8,128)}, bf16[8,32,1280]{2,1,0:T(8,128)(2,1)}, bf16[8,40,1024]{2,1,...) custom-call(f32[32,1280]{1,0:T(8,128)S(1)} %get-tuple-element.45.ref, ...), custom_call_target="tpu_custom_call" | custom-call | tf_op jit(solution)/shard_map/pallas_call | solution.py:505

commit v4 on v3

--- a/solution.py
+++ b/solution.py
@@ -54,14 +54,12 @@
     (
         part0, part1, part2, raw0, raw1, raw2, acc0, acc1, acc2,
         rfac0, rfac1, rfac2,
-        ysend, yrecv, piece, pieces_in, zsend, zrecv, total, fin, colstat,
+        ysend, yrecv, piece, pieces_in, zsend, zrecv, total, fin, ratios, colstat,
         rs_send, rs_recv, ag_send, ag_recv, y_sems, p_sems, z_sems, f_sems,
         *held, load_sems,
     ) = refs[27:]
     grads, masters, rows, columns = held[0:3], held[3:6], held[6:9], held[9:12]
     loads = [pltpu.make_async_copy(given[i], held[i], load_sems.at[i]) for i in range(12)]
-    for load in loads:
-        load.start()
     parts, raws, accs, rfacs = (part0, part1, part2), (raw0, raw1, raw2), (acc0, acc1, acc2), (rfac0, rfac1, rfac2)
 
     k = lax.axis_index("dp")
@@ -84,14 +82,19 @@
 
     barrier = pltpu.get_barrier_semaphore()
 
-    @pl.loop(1, 16)
-    def _(o):
-        pl.semaphore_signal(barrier, inc=1, device_id=z_peer(o), device_id_type=MESH)
+    def far_first(i):
+        return jnp.where(lax.rem(i, 2) == 1, 8 - (i + 1) // 2, 8 + i // 2)
+
+    @pl.loop(0, 15)
+    def _(i):
+        pl.semaphore_signal(barrier, inc=1, device_id=z_peer(far_first(i)), device_id_type=MESH)
 
     @pl.loop(1, 32)
     def _(o):
         pl.semaphore_signal(barrier, inc=1, device_id=plane_peer(o), device_id_type=MESH)
 
+    for load in loads:
+        load.start()
     for load in loads:
         load.wait()
     pl.semaphore_wait(barrier, 46)
@@ -128,33 +131,37 @@
                 for c in (0, 1):
                     raw_copy(m, 7 - s, c).start()
 
-    def forward_first(m, jd):
+    def forward_first(m, jd, c):
         j = real(jd, a)
+        cut = half(m, c)
 
         @pl.when((near == 1) & (jd > near))
         def _():
+            raw_copy(m, jd, c).wait_recv()
+            parts[m][a, j, :, cut] = raws[m][a, j, :, cut].astype(F32) + grads[m][j, :, cut].astype(F32)
+            part_copy(m, a, near, jd, c).start()
+
+        @pl.when((near >= 2) & (jd > near))
+        def _():
+            forward_part(m, a, near, jd, c)
+
+    def forward_part(m, d, here, jd, c):
+        j = real(jd, d)
+        cut = half(m, c)
+        part_copy(m, d, here, jd, c).wait_recv()
+        parts[m][d, j, :, cut] = parts[m][d, j, :, cut] + grads[m][j, :, cut].astype(F32)
+        part_copy(m, d, here, jd, c).start()
+
+    def forward_second(m, r, c):
+        @pl.when((r >= 0) & (7 - r > far))
+        def _():
+            forward_part(m, 1 - a, far, 7 - r, c)
+
+    def forward(ms, u, behind):
+        for m in ms:
             for c in (0, 1):
-                cut = half(m, c)
-                raw_copy(m, jd, c).wait_recv()
-                parts[m][a, j, :, cut] = raws[m][a, j, :, cut].astype(F32) + grads[m][j, :, cut].astype(F32)
-                part_copy(m, a, near, jd, c).start()
-
-        @pl.when((near >= 2) & (jd > near))
-        def _():
-            forward_part(m, a, near, jd)
-
-    def forward_part(m, d, here, jd):
-        j = real(jd, d)
-        for c in (0, 1):
-            cut = half(m, c)
-            part_copy(m, d, here, jd, c).wait_recv()
-            parts[m][d, j, :, cut] = parts[m][d, j, :, cut] + grads[m][j, :, cut].astype(F32)
-            part_copy(m, d, here, jd, c).start()
-
-    def forward_second(m, r):
-        @pl.when((r >= 0) & (7 - r > far))
-        def _():
-            forward_part(m, 1 - a, far, 7 - r)
+                forward_first(m, 7 - u, c)
+                forward_second(m, u - behind, c)
 
     def own_block(m):
         b = 1 - a
@@ -232,9 +239,9 @@
             tile = tile + pieces_in[b, o]
         zsend[b] = tile
 
-        @pl.loop(1, 16)
-        def _(o):
-            z_copy(b, o).start()
+        @pl.loop(0, 15)
+        def _(i):
+            z_copy(b, far_first(i)).start()
 
         colstat[b] = jnp.ones((8, 8, 128), F32)
         for slot, m, lo, hi in LAYOUT[b]:
@@ -243,7 +250,13 @@
                 colstat[b, group - lo, 2 * slot : 2 * slot + 1] = columns[m][cut].reshape(1, 128)
 
     def f_copy(b, o):
-        return remote(fin.at[b, n], fin.at[b, n], f_sems.at[0, b, o], f_sems.at[1, b, o], plane_peer(o))
+        t = lax.rem(p + o, 8)
+        return remote(fin.at[b, p], fin.at[b, p], f_sems.at[0, b, o], f_sems.at[1, b, o], p_peer(t))
+
+    def g_copy(b, i):
+        t = lax.rem(p + lax.rem(i, 8), 8)
+        peer = {"x": t // 2, "core": lax.rem(t, 2), "col": lax.rem(y + i // 8, 4)}
+        return remote(ratios.at[b, 0], ratios.at[b, i], f_sems.at[0, b, i], f_sems.at[1, b, i], peer)
 
     def next_column(old, total_square, m):
         return decay_rate * old + (1.0 - decay_rate) * (total_square / FULL_ROWS[m])
@@ -257,39 +270,61 @@
         for o in range(1, 16):
             tile = tile + zrecv[b, o]
         total[b] = tile
-        fin[b, n] = tile
+        fin[b, p] = tile
+        lane = lax.broadcasted_iota(jnp.int32, (1, 128), 1)
+        marks = jnp.zeros((1, 128), F32)
         for slot, m, lo, hi in LAYOUT[b]:
             plain = total[b, 2 * slot : 2 * slot + 1]
             weighted = total[b, 2 * slot + 1 : 2 * slot + 2]
             new = next_column(colstat[b, p, 2 * slot : 2 * slot + 1], plain, m)
             ratio = jnp.sum(weighted / new, axis=1, keepdims=True)
-            fin[b, n, 2 * slot + 1 : 2 * slot + 2] = jnp.broadcast_to(ratio, (1, 128))
-
-        @pl.loop(1, 32)
+            marks = marks + jnp.where(lane == slot, jnp.broadcast_to(ratio, (1, 128)), 0.0)
+        ratios[b, 0] = marks
+        fin[b, p, 5:6] = marks
+
+        @pl.loop(0, 8)
+        def _(o):
+            g_copy(b, 16 + o).start()
+
+        @pl.loop(0, 8)
+        def _(o):
+            g_copy(b, 8 + o).start()
+            g_copy(b, 24 + o).start()
+
+        @pl.loop(1, 8)
         def _(o):
             f_copy(b, o).start()
 
     def finish(b):
-        @pl.loop(1, 32)
+        @pl.loop(1, 8)
         def _(o):
             f_copy(b, o).wait_recv()
 
-        everyone = fin[b, 0]
-        for which in range(1, 32):
-            everyone = everyone + fin[b, which]
+        @pl.loop(8, 32)
+        def _(i):
+            g_copy(b, i).wait_recv()
+
+        everyone = fin[b, 0, 5:6]
+        for which in range(1, 8):
+            everyone = everyone + fin[b, which, 5:6]
+        for which in range(8, 32):
+            everyone = everyone + ratios[b, which]
+        lane = lax.broadcasted_iota(jnp.int32, (1, 128), 1)
         for m in BATCHES[b]:
             for slot, owner, lo, hi in LAYOUT[b]:
                 if owner != m:
                     continue
                 for group in range(lo, hi):
                     cut = slice(128 * group, 128 * group + 128)
-                    plain = fin[b, y * 8 + (group - lo), 2 * slot : 2 * slot + 1]
+                    plain = fin[b, group - lo, 2 * slot : 2 * slot + 1]
                     columns_next[m][:, cut] = next_column(columns[m][cut].reshape(1, 128), plain, m)
             at_row = 7 - BATCHES[b].index(m)
             row_mean = total[b, at_row : at_row + 1] / FULL_ROWS[m]
-            ratio = sum(
-                everyone[2 * slot + 1 : 2 * slot + 2] for slot, owner, _, _ in LAYOUT[b] if owner == m
-            )
+            mine = [slot for slot, owner, _, _ in LAYOUT[b] if owner == m]
+            chosen = lane == mine[0]
+            for slot in mine[1:]:
+                chosen = chosen | (lane == slot)
+            ratio = jnp.sum(jnp.where(chosen, everyone, 0.0), axis=1, keepdims=True)
             mean_square = row_mean * ratio / (FULL_ROWS[m] * FULL_COLS[m])
             clip = jnp.maximum(1.0, jnp.sqrt(mean_square))
             row_scale = (jnp.sqrt(row_mean) / clip) / jnp.sqrt(rfacs[m][...])
@@ -327,37 +362,30 @@
         send_raw(m)
 
     lag = jnp.where(near == 1, 6, jnp.where(near == 2, 4, 2))
-    lag_pair = jnp.where(near == 1, 4, jnp.where(near == 2, 2, 1))
-
-    @pl.loop(0, 7)
+    lag_pair = jnp.where(near == 1, 6, jnp.where(near == 2, 2, 1))
+
+    @pl.loop(0, 8)
     def _(u):
-        forward_first(0, 7 - u)
-        forward_second(0, u - lag)
-
-    @pl.loop(0, 7)
+        forward((0,), u, lag)
+
+    @pl.loop(0, 8)
     def _(u):
-        for m in (1, 2):
-            forward_first(m, 7 - u)
-        for m in (1, 2):
-            forward_second(m, u - lag_pair)
-
-        @pl.when(u == 0)
+        @pl.when(u == 3 - near)
         def _():
             own_block(0)
             stats_rows(0)
 
-        @pl.when(u == 1)
+        @pl.when(u == 4 - near)
         def _():
             stats_columns(0)
 
-        @pl.when(u == 2)
+        @pl.when(u == 5 - near)
         def _():
             stats_depth(0)
 
-        @pl.when(u == 5)
-        def _():
-            stats_plane(0)
-
+        forward((1, 2), u, lag_pair)
+
+    stats_plane(0)
     for m in (1, 2):
         own_block(m)
     stats_rows(1)
@@ -370,16 +398,16 @@
     gather_step(0, 3)
     stats_plane(1)
     gather_step(0, 4)
+    gather_step(0, 5)
     finish(1)
     for m in (1, 2):
         gather_start(m)
-    gather_step(0, 5)
+    gather_step(0, 6)
     for m in (1, 2):
         gather_step(m, 1)
-    gather_step(0, 6)
+    gather_step(0, 7)
     for m in (1, 2):
         gather_step(m, 2)
-    gather_step(0, 7)
 
     @pl.loop(3, 8)
     def _(s):
@@ -422,9 +450,13 @@
         def _(o):
             z_copy(b, o).wait_send()
 
-        @pl.loop(1, 32)
+        @pl.loop(1, 8)
         def _(o):
             f_copy(b, o).wait_send()
+
+        @pl.loop(8, 32)
+        def _(i):
+            g_copy(b, i).wait_send()
 
 
 def results_kernel(*refs):
@@ -472,7 +504,8 @@
                 pltpu.VMEM((2, 8, 128), F32),
                 pltpu.VMEM((2, 16, 8, 128), F32),
                 pltpu.VMEM((2, 8, 128), F32),
-                pltpu.VMEM((2, 32, 8, 128), F32),
+                pltpu.VMEM((2, 8, 8, 128), F32),
+                pltpu.VMEM((2, 32, 1, 128), F32),
                 pltpu.VMEM((2, 8, 8, 128), F32),
                 dma((3, 2, 8, 2)),
                 dma((3, 2, 8, 2)),

time: 147 us -> 143 us (0.973)
  Pallas kernels: 146 us -> 141 us
    pallas_call x1, Pallas kernels: 144 us -> 139 us  [body(): pl.pallas_call(kernel, out_shape=out_shape, in_specs=[pl.BlockSpec(memory...]
where the time goes in v4:
time: 143 us; the launch traced here: 142 us
  Pallas kernels  141 us (99%)
    pallas_call x1, Pallas kernels, body(): pl.pallas_call(kernel, out_shape=out_shape, in_specs=[pl.BlockSpec(memory...  139 us

profile of v4, /device:TPU:6, one launch (start us, length us, event | category | flops | bytes accessed | tf_op | source)
XLA Modules:
  0.0 141.6 jit_solution(8951559276624252938)
XLA Ops:
  0.7 138.7 %shard_map.235 = (f32[32,1280]{1,0:T(8,128)S(1)}, f32[40,1024]{1,0:T(8,128)S(1)}, f32[32,1024]{1,0:T(8,128)S(1)}, bf16[8,32,1280]{2,1,0:T(8,128)(2,1)S(1)}, bf16...) custom-call(bf16[8,32,1280]{2,1,0:T(8,128)(2,1)} %bitcast.6, ...), custom_call_target="tpu_custom_call" | custom-call | tf_op jit(solution)/shard_map/pallas_call | solution.py:489
  139.4 2.3 %shard_map.236 = (f32[32,1280]{1,0:T(8,128)}, f32[40,1024]{1,0:T(8,128)}, f32[32,1024]{1,0:T(8,128)}, bf16[8,32,1280]{2,1,0:T(8,128)(2,1)}, bf16[8,40,1024]{2,1,...) custom-call(f32[32,1280]{1,0:T(8,128)S(1)} %get-tuple-element.45.ref, ...), custom_call_target="tpu_custom_call" | custom-call | tf_op jit(solution)/shard_map/pallas_call | solution.py:538

commit v5 on v4

--- a/solution.py
+++ b/solution.py
@@ -395,21 +395,23 @@
     gather_step(0, 1)
     stats_depth(1)
     gather_step(0, 2)
+    stats_plane(1)
     gather_step(0, 3)
-    stats_plane(1)
     gather_step(0, 4)
-    gather_step(0, 5)
     finish(1)
     for m in (1, 2):
         gather_start(m)
+    gather_step(0, 5)
+    for m in (1, 2):
+        gather_step(m, 1)
     gather_step(0, 6)
     for m in (1, 2):
-        gather_step(m, 1)
+        gather_step(m, 2)
     gather_step(0, 7)
     for m in (1, 2):
-        gather_step(m, 2)
-
-    @pl.loop(3, 8)
+        gather_step(m, 3)
+
+    @pl.loop(4, 8)
     def _(s):
         for m in (1, 2):
             gather_step(m, s)

time: 143 us -> 140 us (0.979)
  Pallas kernels: 141 us -> 138 us
    pallas_call x1, Pallas kernels: 139 us -> 136 us  [body(): pl.pallas_call(kernel, out_shape=out_shape, in_specs=[pl.BlockSpec(memory...]
where the time goes in v5:
time: 140 us; the launch traced here: 139 us
  Pallas kernels  138 us (99%)
    pallas_call x1, Pallas kernels, body(): pl.pallas_call(kernel, out_shape=out_shape, in_specs=[pl.BlockSpec(memory...  136 us

profile of v5, /device:TPU:6, one launch (start us, length us, event | category | flops | bytes accessed | tf_op | source)
XLA Modules:
  0.0 139.1 jit_solution(18160545001389115507)
XLA Ops:
  0.7 136.2 %shard_map.235 = (f32[32,1280]{1,0:T(8,128)S(1)}, f32[40,1024]{1,0:T(8,128)S(1)}, f32[32,1024]{1,0:T(8,128)S(1)}, bf16[8,32,1280]{2,1,0:T(8,128)(2,1)S(1)}, bf16...) custom-call(bf16[8,32,1280]{2,1,0:T(8,128)(2,1)} %bitcast.6, ...), custom_call_target="tpu_custom_call" | custom-call | tf_op jit(solution)/shard_map/pallas_call | solution.py:491
  136.9 2.3 %shard_map.236 = (f32[32,1280]{1,0:T(8,128)}, f32[40,1024]{1,0:T(8,128)}, f32[32,1024]{1,0:T(8,128)}, bf16[8,32,1280]{2,1,0:T(8,128)(2,1)}, bf16[8,40,1024]{2,1,...) custom-call(f32[32,1280]{1,0:T(8,128)S(1)} %get-tuple-element.45.ref, ...), custom_call_target="tpu_custom_call" | custom-call | tf_op jit(solution)/shard_map/pallas_call | solution.py:540

commit v6 on v5

--- a/solution.py
+++ b/solution.py
@@ -334,6 +334,7 @@
             new = masters[m][...] - learn_rate * step
             updated[m][...] = new
             weights[m][k] = new.astype(BF16)
+            gather_start(m)
 
     def w_copy(m, d, i):
         to = jnp.clip(k + 1 - 2 * d, 0, 7)
@@ -390,7 +391,6 @@
         own_block(m)
     stats_rows(1)
     finish(0)
-    gather_start(0)
     stats_columns(1)
     gather_step(0, 1)
     stats_depth(1)
@@ -399,8 +399,6 @@
     gather_step(0, 3)
     gather_step(0, 4)
     finish(1)
-    for m in (1, 2):
-        gather_start(m)
     gather_step(0, 5)
     for m in (1, 2):
         gather_step(m, 1)

time: 140 us -> 140 us (level)
  no operation moved by 1% of the time
where the time goes in v6:
time: 140 us; the launch traced here: 139 us
  Pallas kernels  138 us (99%)
    pallas_call x1, Pallas kernels, body(): pl.pallas_call(kernel, out_shape=out_shape, in_specs=[pl.BlockSpec(memory...  136 us

profile of v6, /device:TPU:6, one launch (start us, length us, event | category | flops | bytes accessed | tf_op | source)
XLA Modules:
  0.0 139.1 jit_solution(12794339210895765405)
XLA Ops:
  0.7 136.2 %shard_map.235 = (f32[32,1280]{1,0:T(8,128)S(1)}, f32[40,1024]{1,0:T(8,128)S(1)}, f32[32,1024]{1,0:T(8,128)S(1)}, bf16[8,32,1280]{2,1,0:T(8,128)(2,1)S(1)}, bf16...) custom-call(bf16[8,32,1280]{2,1,0:T(8,128)(2,1)} %bitcast.6, ...), custom_call_target="tpu_custom_call" | custom-call | tf_op jit(solution)/shard_map/pallas_call | solution.py:489
  136.9 2.3 %shard_map.236 = (f32[32,1280]{1,0:T(8,128)}, f32[40,1024]{1,0:T(8,128)}, f32[32,1024]{1,0:T(8,128)}, bf16[8,32,1280]{2,1,0:T(8,128)(2,1)}, bf16[8,40,1024]{2,1,...) custom-call(f32[32,1280]{1,0:T(8,128)S(1)} %get-tuple-element.45.ref, ...), custom_call_target="tpu_custom_call" | custom-call | tf_op jit(solution)/shard_map/pallas_call | solution.py:538
